TPU v7x, 512 devices: a 4x2x32 block of a 4x8x32 slice. The times are simulated.
512 devices in a mesh: groups: 2 (over y), trades: 32 (over z), scen: 4 (over x), fact: 2 (over core).
Axes of the slice: x: 4, y: 2, z: 32, core: 2. Of those that a mesh axis runs over, the one named last changes fastest.
The devices are a block of a 4x8x32 slice.
Arguments:
- scenario_state: bfloat16 [256, 256], P(('groups', 'scen')), parts along dimension 0, may hold values from -6 to 6
- direction: bfloat16 [16384, 256], P('trades'), may hold values from -0.375 to 0.375
- trade_load: bfloat16 [16384, 256], P('trades', 'fact'), may hold values from -6 to 6
- trade_curve: bfloat16 [16384, 256], P('trades', 'fact'), may hold values from -3 to 3
- trade_set: int32 [16384], P('trades'), may hold values from 0 to 127, as said below
- factor_bucket_index: int32 [256], P('fact'), may hold values from 0 to 11
- threshold: float32 [12], replicated, may hold values from 5 to 500
- factor_risk_weight: float32 [256], P('fact'), may hold values from 0.5 to 2
- correlation: float32 [256, 256], P(None, 'fact'), may hold values from -1 to 1, as said below
- funding: float32 [256, 128], P(('groups', 'scen')), parts along dimension 0, may hold values from 0.05 to 0.5
Outputs:
- state_grad: float32 [256, 256], P(('groups', 'scen'), 'fact'), parts along dimension 0
- weight_grad: float32 [512], P(('groups', 'fact')), parts along dimension 0
There are 2 independent parts, one for each index of `groups`. A program takes and returns all parts, laid end to end along the dimension named above; an argument that names none is the same for every part. Nothing has to cross between parts.
Inputs may be any that keep to these rules, and one draw needn't show every extreme that they name: `trade_set`: never falling along the trades; set 0 begins at trade 0, and set n begins at a trade of n * 128 to (n + 1) * 128 - 1. `correlation`: symmetric positive definite with unit diagonal.
All inputs are finite; a program needn't handle non-finite values.
Results may differ from a plain program's by a relative error of at most 0.009.
Values may be sent and summed in bfloat16 or wider, within the bound.
No kernel may reach another device: no remote copies, remote signals or barrier semaphores. Data moves between devices by JAX's collectives and lax.ppermute only.
A program may use at most 64 MiB of HBM per device.

v0:
```python
import jax
import jax.numpy as jnp
from jax import lax
from jax.sharding import PartitionSpec as P

NSET_DEV = 4


def copy_for_each(x, axis):
    copies = jnp.broadcast_to(x, (lax.axis_size(axis), *x.shape))
    return lax.all_to_all(copies, axis, split_axis=0, concat_axis=0, tiled=True)


def of_everyone(x, axis):
    return copy_for_each(x, axis).sum(axis=0)


def cut_along(x, dim, size):
    dims = x.shape
    tiles = x.reshape(*dims[:dim], size, dims[dim] // size, *dims[dim + 1 :])
    return jnp.moveaxis(tiles, dim, 0)


def sum_at_owner(x, axis, dim):
    size = lax.axis_size(axis)
    tiles = lax.all_to_all(cut_along(x, dim, size), axis, 0, 0, tiled=True)
    return jnp.sum(tiles, axis=0)


def of_everyone_2(x, axis):
    return copy_for_each(x, axis).astype(jnp.float32).sum(axis=0)


def shifted(x, axis, by):
    size = lax.axis_size(axis)
    pairs = [(i, i + by) for i in range(size) if 0 <= i + by < size]
    return lax.ppermute(x, axis, pairs)


def over_axes(x, axes):
    far, near = axes
    return of_everyone(of_everyone(x, near), far)


def total_of_pieces(x, axis):
    return lax.all_gather(x, axis).sum(0)


def initial_margin_reverse(
    netted_sensitivity,
    local_funding_cost,
    factor_bucket_index,
    threshold,
    factor_risk_weight,
    correlation,
):
    precise = lax.Precision.HIGHEST
    set_here, scen_here, factor_half = netted_sensitivity.shape
    bucket_hot = (
        factor_bucket_index[:, None] == jnp.arange(threshold.shape[0], dtype=jnp.int32)[None, :]
    ).astype(jnp.float32)
    bucket_part = jnp.einsum("nsk,kb->nsb", netted_sensitivity, bucket_hot, precision=precise)
    bucket_sum = of_everyone(bucket_part, "fact")
    raw_ratio = jnp.sqrt(jnp.abs(bucket_sum) / threshold)
    concentration = jnp.maximum(jnp.float32(1.0), raw_ratio)
    conc_factor = jnp.einsum("nsb,kb->nsk", concentration, bucket_hot, precision=precise)
    weighted = factor_risk_weight * netted_sensitivity * conc_factor
    weighted_cols = weighted.reshape(set_here * scen_here, factor_half).T
    image_cols = sum_at_owner(jnp.dot(correlation, weighted_cols, precision=precise), "fact", 0)
    corr_image = image_cols.T.reshape(set_here, scen_here, factor_half)
    margin_sq = of_everyone(jnp.sum(weighted * corr_image, -1), "fact")
    margin = jnp.sqrt(margin_sq + 1e-06)
    weighted_bar = (local_funding_cost / margin)[..., None] * corr_image
    conc_part = jnp.einsum(
        "nsk,kb->nsb",
        weighted_bar * factor_risk_weight * netted_sensitivity,
        bucket_hot,
        precision=precise,
    )
    conc_bar = of_everyone_2(conc_part.astype(jnp.bfloat16), "fact").astype(jnp.float32)
    bucket_bar = jnp.where(
        raw_ratio > 1.0,
        conc_bar * jnp.sign(bucket_sum) / (2.0 * threshold * concentration),
        jnp.float32(0.0),
    )
    spread_bar = jnp.einsum("nsb,kb->nsk", bucket_bar, bucket_hot, precision=precise)
    netted_sensitivity_bar = (weighted_bar * factor_risk_weight * conc_factor + spread_bar).astype(
        jnp.bfloat16
    )
    weight_row_table = jnp.sum(weighted_bar * netted_sensitivity * conc_factor, axis=1)
    return (netted_sensitivity_bar, weight_row_table)


def on_device(
    scenario_state,
    direction,
    trade_load,
    trade_curve,
    trade_set,
    factor_bucket_index,
    threshold,
    factor_risk_weight,
    correlation,
    funding,
):
    scen_here = scenario_state.shape[0]
    trade_here = direction.shape[0]
    factor_half = trade_load.shape[1]
    set_count = funding.shape[1]
    owned = NSET_DEV
    span = owned + 1
    position = lax.axis_index("trades")
    first_set = position * owned
    window_base = first_set - 1
    moneyness = jnp.einsum(
        "sk,tk->st", scenario_state, direction, preferred_element_type=jnp.float32
    )
    likely = jax.nn.sigmoid(moneyness)
    paired = jnp.concatenate([likely.astype(jnp.bfloat16), moneyness.astype(jnp.bfloat16)], axis=1)
    window_rows = jnp.arange(span, dtype=jnp.int32)
    member = ((trade_set - window_base)[None, :] == window_rows[:, None]).astype(jnp.bfloat16)
    member_two = jnp.concatenate([member, member], axis=1)
    stacked = jnp.concatenate([trade_load, trade_curve], axis=0)
    mixing = member_two[:, None, :] * paired[None, :, :]
    window_net = jnp.einsum("wst,tk->wsk", mixing, stacked, preferred_element_type=jnp.float32)
    local_funding_cost = lax.dynamic_slice_in_dim(funding, first_set, owned, 1).T
    passed = shifted(window_net[0], "trades", -1)
    extra = jnp.concatenate(
        [jnp.zeros((owned - 1, scen_here, factor_half), jnp.float32), passed[None]], axis=0
    )
    netted_sensitivity = window_net[1:] + extra
    netted_sensitivity_bar, weight_row_table = initial_margin_reverse(
        netted_sensitivity,
        local_funding_cost,
        factor_bucket_index,
        threshold,
        factor_risk_weight,
        correlation,
    )
    carried = shifted(netted_sensitivity_bar[owned - 1], "trades", 1)
    window_bar = jnp.concatenate([carried[None], netted_sensitivity_bar], axis=0)
    weight_sum = over_axes(jnp.sum(weight_row_table, 0), ("trades", "scen"))
    spread = jnp.einsum("wsk,tk->wst", window_bar, stacked, preferred_element_type=jnp.float32)
    pulled = jnp.sum(spread * member_two.astype(jnp.float32)[:, None, :], 0)
    pulled = of_everyone(pulled, "fact")
    money_bar = (pulled[:, :trade_here] * likely * (1.0 - likely) + pulled[:, trade_here:]).astype(
        jnp.bfloat16
    )
    direction_half = lax.dynamic_slice_in_dim(
        direction, lax.axis_index("fact") * factor_half, factor_half, 1
    )
    state_part = jnp.dot(money_bar, direction_half, preferred_element_type=jnp.float32)
    state_grad = total_of_pieces(state_part, "trades")
    weight_grad = weight_sum / (scen_here * lax.axis_size("scen") * set_count)
    return (state_grad, weight_grad)


def solution(mesh):
    placed = (
        P(("groups", "scen"), None),
        P("trades", None),
        P("trades", "fact"),
        P("trades", "fact"),
        P("trades"),
        P("fact"),
        P(),
        P("fact"),
        P(None, "fact"),
        P(("groups", "scen"), None),
    )
    return jax.shard_map(
        on_device,
        mesh=mesh,
        in_specs=placed,
        out_specs=(P(("groups", "scen"), "fact"), P(("groups", "fact"))),
        check_vma=False,
    )
```

profile of v0, /device:TPU:40, one launch (start us, length us, event | category | flops | bytes accessed | tf_op | source)
XLA Modules:
  0.0 154.9 jit_solution(10648227106633272902)
XLA Ops:
  0.7 0.7 copy-done.6
  1.6 0.5 copy-done.9
  2.4 0.7 copy-done.8
  3.5 1.3 collective-permute-start
  4.9 0.6 copy-done.5
  5.7 4.3 %collective-permute-done = f32[32,128]{1,0:T(8,128)S(1)} collective-permute-done((f32[32,128]{1,0:T(8,128)S(1)}, f32[32,128]{1,0:T(8,128)S(1)}, u32[]{:S(2)}, u32[]{:S(2)}) %collective-permute-start) | collective-permute-done | bytes 16416 | tf_op jit(solution)/shard_map/ppermute | solution.py:37
  10.3 3.7 %all_to_all.37 = f32[2,1,1536]{2,1,0:T(1,128)S(1)} all-to-all(f32[2,1,1536]{2,1,0:T(1,128)S(1)} %reshape.55), channel_id=1, replica_groups=mesh['groups'=2,'trades'=32,'scen'=4,'fact'=2] {'fact'}, dimensions={0} | all-to-all | bytes 24576 | tf_op jit(solution)/shard_map/all_to_all | solution.py:11
  14.6 0.7 reduce.3
  15.5 0.5 copy-done.4
  16.3 0.7 copy-done.1
  17.3 3.9 %all_to_all.38 = f32[2,128,128]{1,2,0:T(8,128)S(1)} all-to-all(f32[2,128,128]{1,2,0:T(8,128)S(1)} %bitcast.51), channel_id=1, replica_groups=mesh['groups'=2,'trades'=32,'scen'=4,'fact'=2] {'fact'}, dimensions={0} | all-to-all | bytes 262144 | tf_op jit(solution)/shard_map/all_to_all | solution.py:26
  21.3 3.7 %all_to_all.39 = f32[2,1,128]{2,1,0:T(1,128)S(1)} all-to-all(f32[2,1,128]{2,1,0:T(1,128)S(1)} %reshape.57), channel_id=1, replica_groups=mesh['groups'=2,'trades'=32,'scen'=4,'fact'=2] {'fact'}, dimensions={0} | all-to-all | bytes 2048 | tf_op jit(solution)/shard_map/all_to_all | solution.py:11
  25.0 0.7 reduce.4
  26.3 3.7 %all_to_all.40 = bf16[2,2,768]{2,1,0:T(2,128)(2,1)S(1)} all-to-all(bf16[2,2,768]{2,1,0:T(2,128)(2,1)S(1)} %reshape.59), channel_id=1, replica_groups=mesh['groups'=2,'trades'=32,'scen'=4,'fact'=2] {'fact'}, dimensions={0} | all-to-all | bytes 12288 | tf_op jit(solution)/shard_map/all_to_all | solution.py:11
  30.5 4.7 %collective-permute-start.1 = (bf16[32,128]{1,0:T(8,128)(2,1)S(1)}, bf16[32,128]{1,0:T(8,128)(2,1)S(1)}, u32[]{:S(2)}, u32[]{:S(2)}) collective-permute-start(bf16[32,128]{1,0:T(8,128)(2,1)S(1)} %slice_bitcast_fusion.1), channel_id=1, source_target_pairs={{0,8},{8,16},{16,24},{24,32},{32,40},{40,48},{48,56},{56,64},{64,7... | collective-permute-start | bytes 24584 | tf_op jit(solution)/shard_map/ppermute | solution.py:37
  35.3 0.6 broadcast_in_dim.49
  35.9 4.6 %all-to-all-start.5 = ((f32[4,1,128]{2,1,0:T(1,128)}), f32[4,1,128]{2,1,0:T(1,128)S(1)}, u32[]{:S(2)}, u32[]{:S(2)}) async-start(f32[4,1,128]{2,1,0:T(1,128)} %broadcast_in_dim.49), calls=%async_computation.5 | async-start | bytes 4096 | tf_op jit(solution)/shard_map/all_to_all | solution.py:11
  40.5 5.2 %all-to-all-done.5 = f32[4,1,128]{2,1,0:T(1,128)S(1)} async-done(((f32[4,1,128]{2,1,0:T(1,128)}), f32[4,1,128]{2,1,0:T(1,128)S(1)}, u32[]{:S(2)}, u32[]{:S(2)}) %all-to-all-start.5) | async-done | bytes 2080 | tf_op jit(solution)/shard_map/all_to_all | solution.py:11
  46.0 4.0 %all_to_all.41 = f32[2,32,1024]{2,1,0:T(8,128)S(1)} all-to-all(f32[2,32,1024]{2,1,0:T(8,128)S(1)} %broadcast_in_dim.48), channel_id=1, replica_groups=mesh['groups'=2,'trades'=32,'scen'=4,'fact'=2] {'fact'}, dimensions={0} | all-to-all | bytes 524288 | tf_op jit(solution)/shard_map/all_to_all | solution.py:11
  49.9 0.6 broadcast_in_dim.50
  50.5 44.5 %all-to-all-start.6 = ((f32[32,1,128]{2,1,0:T(1,128)}), f32[32,1,128]{2,1,0:T(1,128)S(1)}, u32[]{:S(2)}, u32[]{:S(2)}) async-start(f32[32,1,128]{2,1,0:T(1,128)} %broadcast_in_dim.50), calls=%async_computation.6 | async-start | bytes 32768 | tf_op jit(solution)/shard_map/all_to_all | solution.py:11
  95.2 58.5 %all-gather = f32[1024,128]{1,0:T(8,128)S(1)} all-gather(f32[32,128]{1,0:T(8,128)S(1)} %fusion.6), channel_id=2, replica_groups=mesh['groups'=2,'trades'=32,'scen'=4,'fact'=2] {'trades'}, dimensions={0}, use_global_device_ids=true | all-gather | bytes 540672 | tf_op jit(solution)/shard_map/all_gather | solution.py:46
  153.7 0.6 reduce_sum.110
  154.4 0.5 broadcast_multiply_fusion
  (60 shorter events, 4.5 us)
Async XLA Ops:
  0.6 1.0 copy-start
  0.7 0.7 copy-start.6
  1.4 0.7 copy-start.9
  2.1 0.9 copy-start.8
  2.3 0.9 copy-start.7
  3.5 2.0 %copy-start.2 = (f32[32,128]{1,0:T(8,128)S(1)}, f32[32,128]{1,0:T(8,128)}, u32[]{:S(2)}) copy-start(f32[32,128]{1,0:T(8,128)} %param.19) | copy-start | bytes 49156
  3.5 6.4 %collective-permute-start = (f32[32,128]{1,0:T(8,128)S(1)}, f32[32,128]{1,0:T(8,128)S(1)}, u32[]{:S(2)}, u32[]{:S(2)}) collective-permute-start(f32[32,128]{1,0:T(8,128)S(1)} %slice_bitcast_fusion), channel_id=1, source_target_pairs={{8,0},{16,8},{24,16},{32,24},{40,32},{48,40},{56,48},{64,56},{72,6... | collective-permute-start | bytes 49160 | tf_op jit(solution)/shard_map/ppermute | solution.py:37
  4.8 0.7 copy-start.5
  5.7 4.3 %copy-start.3 = (s32[128]{0:T(128)S(1)}, s32[128]{0:T(128)}, u32[]{:S(2)}) copy-start(s32[128]{0:T(128)} %param.15) | copy-start | bytes 1540
  15.4 0.7 copy-start.4
  16.1 0.9 copy-start.1
  30.5 15.2 %collective-permute-start.1 = (bf16[32,128]{1,0:T(8,128)(2,1)S(1)}, bf16[32,128]{1,0:T(8,128)(2,1)S(1)}, u32[]{:S(2)}, u32[]{:S(2)}) collective-permute-start(bf16[32,128]{1,0:T(8,128)(2,1)S(1)} %slice_bitcast_fusion.1), channel_id=1, source_target_pairs={{0,8},{8,16},{16,24},{24,32},{32,40},{40,48},{48,56},{56,64},{64,7... | collective-permute-start | bytes 24584 | tf_op jit(solution)/shard_map/ppermute | solution.py:37
  35.9 9.8 %all-to-all-start.5 = ((f32[4,1,128]{2,1,0:T(1,128)}), f32[4,1,128]{2,1,0:T(1,128)S(1)}, u32[]{:S(2)}, u32[]{:S(2)}) async-start(f32[4,1,128]{2,1,0:T(1,128)} %broadcast_in_dim.49), calls=%async_computation.5 | async-start | bytes 4096 | tf_op jit(solution)/shard_map/all_to_all | solution.py:11
  50.5 103.8 %all-to-all-start.6 = ((f32[32,1,128]{2,1,0:T(1,128)}), f32[32,1,128]{2,1,0:T(1,128)S(1)}, u32[]{:S(2)}, u32[]{:S(2)}) async-start(f32[32,1,128]{2,1,0:T(1,128)} %broadcast_in_dim.50), calls=%async_computation.6 | async-start | bytes 32768 | tf_op jit(solution)/shard_map/all_to_all | solution.py:11
where the time goes:
time: 155 us
  blocking collectives  77.5 us (50%)
  starting transfers between devices  55.1 us (36%)
  waiting for transfers between devices  9.5 us (6%)
  local copies, waits for them, and re-layouts  6.72 us (4%)
  other arithmetic  3.08 us (2%)
  matrix products  2.15 us (1%)
    all_gather x1, blocking collectives, total_of_pieces(): return lax.all_gather(x, axis).sum(0)  58.5 us
    all_to_all x2, starting transfers between devices, copy_for_each(): return lax.all_to_all(copies, axis, split_axis=0, concat_axis=0, tiled=True)  49 us
    all_to_all x4, blocking collectives, copy_for_each(): return lax.all_to_all(copies, axis, split_axis=0, concat_axis=0, tiled=True)  15.1 us
    ppermute x2, starting transfers between devices, shifted(): return lax.ppermute(x, axis, pairs)  6.02 us
    all_to_all x2, waiting for transfers between devices, copy_for_each(): return lax.all_to_all(copies, axis, split_axis=0, concat_axis=0, tiled=True)  5.21 us
    unnamed x29, local copies, waits for them, and re-layouts  4.84 us
    ppermute x2, waiting for transfers between devices, shifted(): return lax.ppermute(x, axis, pairs)  4.29 us
    all_to_all x1, blocking collectives, sum_at_owner(): tiles = lax.all_to_all(cut_along(x, dim, size), axis, 0, 0, tiled=True)  3.85 us
  transfers between devices with their start and end apart: 4, of which 2 were waited for; matrix products, arithmetic and copies ran while one was open for 1% of the time, Pallas kernels for 0%

commit v1 on v0

v1 whole, which is shorter than its diff:
```python
import jax
import jax.numpy as jnp
from jax import lax
from jax.experimental import pallas as pl
from jax.experimental.pallas import tpu as pltpu
from jax.sharding import PartitionSpec as P

NSET_DEV = 4
SPAN = NSET_DEV + 1
NEAR = 4
F32 = jnp.float32
BF16 = jnp.bfloat16
PRECISE = lax.Precision.HIGHEST


def three_parts(x):
    high = x.astype(BF16)
    rest = x - high.astype(F32)
    mid = rest.astype(BF16)
    low = (rest - mid.astype(F32)).astype(BF16)
    return high, mid, low


def from_parts(high, mid, low):
    return high.astype(F32) + mid.astype(F32) + low.astype(F32)


def dot_t(a, b, **kw):
    return lax.dot_general(a, b, (((1,), (1,)), ((), ())), preferred_element_type=F32, **kw)


def dot(a, b, **kw):
    return lax.dot_general(a, b, (((1,), (0,)), ((), ())), preferred_element_type=F32, **kw)


def pack_kernel(load, curve, corr, small, out):
    trades, half = load.shape
    start = pl.multiple_of(lax.axis_index("fact") * half, half)
    out[:trades] = load[...]
    out[trades : 2 * trades] = curve[...]
    parts = three_parts(corr[pl.ds(start, half)])
    for i, part in enumerate(parts):
        out[2 * trades + i * half : 2 * trades + (i + 1) * half] = part
    parts = three_parts(small[...])
    base = 2 * trades + 3 * half
    for i, part in enumerate(parts):
        out[base + 8 * i : base + 8 * (i + 1)] = part


def money_kernel(state, direction, money_out, pair_out):
    money = dot_t(state[...], direction[...])
    money_out[...] = money
    trades = direction.shape[0]
    pair_out[:, :trades] = lax.logistic(money).astype(BF16)
    pair_out[:, trades:] = money.astype(BF16)


def window_kernel(pair, sets, mine, other, net_out):
    scen, double = pair.shape
    trades = double // 2
    first = lax.axis_index("trades") * NSET_DEV - 1
    paired = pair[...]
    where_set = jnp.concatenate([sets[...], sets[...]], axis=1) - first
    half = mine.shape[1]
    own = mine[:double]
    swapped = other[:double]
    for w in range(SPAN):
        member = jnp.where(where_set == w, 1.0, 0.0).astype(BF16)
        mixing = paired * member
        net_out[w * scen : (w + 1) * scen, :half] = dot(mixing, own)
        net_out[w * scen : (w + 1) * scen, half:] = dot(mixing, swapped)


def sets_kernel(
    net, above, below, money, sets, mine, other, corr, threshold, fund, direction,
    state_out, weight_out,
):
    rows, factors = net.shape
    scen = rows // SPAN
    double = 2 * direction.shape[0]
    trades = direction.shape[0]
    half = factors // 2
    side = pl.multiple_of(lax.axis_index("fact") * half, half)
    far_side = pl.multiple_of((1 - lax.axis_index("fact")) * half, half)
    netted = jnp.concatenate(
        [
            net[:scen] + above[...],
            net[scen : (SPAN - 1) * scen],
            net[(SPAN - 1) * scen :] + below[...],
        ],
        axis=0,
    )
    base = double + 3 * half

    def row_of(ref, i):
        return from_parts(ref[base + i : base + i + 1], ref[base + 8 + i : base + 9 + i], ref[base + 16 + i : base + 17 + i])

    risk = jnp.concatenate([row_of(mine, 0), row_of(other, 0)], axis=1)
    bucket = jnp.concatenate([row_of(mine, 1), row_of(other, 1)], axis=1).astype(jnp.int32)
    buckets = threshold.shape[1]
    hot = jnp.where(
        lax.broadcasted_iota(jnp.int32, (buckets, factors), 0) == bucket, 1.0, 0.0
    ).astype(F32)
    limit = threshold[...]
    bucket_sum = dot_t(netted, hot, precision=PRECISE)
    raw_ratio = jnp.sqrt(jnp.abs(bucket_sum) / limit)
    concentration = jnp.maximum(1.0, raw_ratio)
    conc_factor = dot(concentration, hot, precision=PRECISE)
    scaled = risk * conc_factor
    weighted = scaled * netted
    near_cols = corr[pl.ds(side, half)]
    cross = corr[pl.ds(far_side, half)]
    far_cols = from_parts(*[other[double + i * half : double + (i + 1) * half] for i in range(3)])
    w_own, w_far = weighted[:, :half], weighted[:, half:]
    image = jnp.concatenate(
        [
            dot(w_own, near_cols, precision=PRECISE) + dot(w_far, cross, precision=PRECISE),
            dot_t(w_own, cross, precision=PRECISE) + dot(w_far, far_cols, precision=PRECISE),
        ],
        axis=1,
    )
    margin = jnp.sqrt(jnp.sum(weighted * image, axis=1, keepdims=True) + 1e-06)
    weighted_bar = (fund[...] / margin) * image
    conc_bar = dot_t(weighted_bar * risk * netted, hot, precision=PRECISE)
    sign = jnp.where(bucket_sum > 0.0, 1.0, jnp.where(bucket_sum < 0.0, -1.0, 0.0))
    bucket_bar = jnp.where(raw_ratio > 1.0, conc_bar * sign / (2.0 * limit * concentration), 0.0)
    bar = (weighted_bar * scaled + dot(bucket_bar, hot, precision=PRECISE)).astype(BF16)
    grad_terms = weighted_bar[scen:] * netted[scen:] * conc_factor[scen:]
    weight_out[...] = jnp.broadcast_to(jnp.sum(grad_terms[:, :half], axis=0, keepdims=True), weight_out.shape)
    spread = dot_t(bar[:, :half], mine[:double]) + dot_t(bar[:, half:], other[:double])
    first = lax.axis_index("trades") * NSET_DEV - 1
    where_set = jnp.concatenate([sets[...], sets[...]], axis=1) - first
    pulled = jnp.zeros((scen, double), F32)
    for w in range(SPAN):
        pulled = pulled + jnp.where(where_set == w, spread[w * scen : (w + 1) * scen], 0.0)
    likely = lax.logistic(money[...])
    money_bar = (pulled[:, :trades] * likely * (1.0 - likely) + pulled[:, trades:]).astype(BF16)
    state_out[...] = dot(money_bar, direction[:, pl.ds(side, half)])


def call(body, out_shape, *args):
    return pl.pallas_call(
        body,
        out_shape=out_shape,
        in_specs=[pl.BlockSpec(memory_space=pltpu.VMEM)] * len(args),
        out_specs=jax.tree.map(lambda _: pl.BlockSpec(memory_space=pltpu.VMEM), out_shape),
    )(*args)


def shifted(x, axis, by):
    size = lax.axis_size(axis)
    pairs = [(i, i + by) for i in range(size) if 0 <= i + by < size]
    return lax.ppermute(x, axis, pairs)


def exchange(pieces, axes, groups):
    return lax.all_to_all(pieces, axes, 0, 0, tiled=True, axis_index_groups=groups)


def reduce_over_trades(state_part, weight_part):
    devs, cols = lax.axis_size("trades"), lax.axis_size("scen")
    scen, half = state_part.shape
    blocks = devs // NEAR
    rows = scen // NEAR
    near = [
        [(b * NEAR + j) * cols + c for j in range(NEAR) for c in range(cols)]
        for b in range(blocks)
    ]
    pieces = jnp.concatenate(
        [
            state_part.reshape(NEAR, rows * half),
            jnp.broadcast_to(weight_part.reshape(1, half), (NEAR, half)),
        ],
        axis=1,
    ).astype(BF16)
    length = (rows + 1) * half
    pieces = jnp.broadcast_to(pieces[:, None, None], (NEAR, cols, 1, length)).reshape(NEAR * cols, 1, length)
    got = exchange(pieces, ("trades", "scen"), near).reshape(NEAR, cols, length).astype(F32)
    state = lax.dynamic_index_in_dim(got, lax.axis_index("scen"), 1, keepdims=False)
    state = jnp.sum(state[:, : rows * half], axis=0)
    weight = jnp.sum(got[:, :, rows * half :], axis=(0, 1))
    far = [[b * NEAR + j for b in range(blocks)] for j in range(NEAR)]
    piece = jnp.concatenate([state, weight]).astype(BF16)
    pieces = jnp.broadcast_to(piece[None, None], (blocks, 1, length))
    total = jnp.sum(exchange(pieces, "trades", far).reshape(blocks, length).astype(F32), axis=0)
    weight = total[rows * half :]
    group = [[b * NEAR + j for j in range(NEAR)] for b in range(blocks)]
    pieces = jnp.broadcast_to(total[None, None, : rows * half].astype(BF16), (NEAR, 1, rows * half))
    state = exchange(pieces, "trades", group).reshape(scen, half).astype(F32)
    return state, weight


def on_device(
    scenario_state,
    direction,
    trade_load,
    trade_curve,
    trade_set,
    factor_bucket_index,
    threshold,
    factor_risk_weight,
    correlation,
    funding,
):
    scen, set_count = funding.shape
    trades, half = trade_load.shape
    double, factors = 2 * trades, 2 * half
    small = jnp.zeros((8, half), F32)
    small = small.at[0].set(factor_risk_weight).at[1].set(factor_bucket_index.astype(F32))
    mine = call(
        pack_kernel,
        jax.ShapeDtypeStruct((double + 3 * half + 24, half), BF16),
        trade_load, trade_curve, correlation, small,
    )
    other = lax.ppermute(mine, "fact", [(0, 1), (1, 0)])
    money, pair = call(
        money_kernel,
        (jax.ShapeDtypeStruct((scen, trades), F32), jax.ShapeDtypeStruct((scen, double), BF16)),
        scenario_state, direction,
    )
    sets = trade_set.reshape(1, trades)
    net = call(
        window_kernel,
        jax.ShapeDtypeStruct((SPAN * scen, factors), F32),
        pair, sets, mine, other,
    )
    below = shifted(net[:scen], "trades", -1)
    above = shifted(net[(SPAN - 1) * scen :], "trades", 1)
    first = lax.axis_index("trades") * NSET_DEV - 1
    padded = jnp.concatenate([funding[:, :1], funding], axis=1)
    fund = lax.dynamic_slice_in_dim(padded, first + 1, SPAN, 1).T.reshape(SPAN * scen, 1)
    buckets = threshold.shape[0]
    limit = jnp.concatenate([threshold, jnp.ones((-buckets % 16,), F32)]).reshape(1, -1)
    state_part, weight_part = call(
        sets_kernel,
        (jax.ShapeDtypeStruct((scen, half), F32), jax.ShapeDtypeStruct((8, half), F32)),
        net, above, below, money, sets, mine, other, correlation, limit, fund, direction,
    )
    state_grad, weight_sum = reduce_over_trades(state_part, weight_part[:1])
    weight_grad = weight_sum / (scen * lax.axis_size("scen") * set_count)
    return (state_grad, weight_grad)


def solution(mesh):
    placed = (
        P(("groups", "scen"), None),
        P("trades", None),
        P("trades", "fact"),
        P("trades", "fact"),
        P("trades"),
        P("fact"),
        P(),
        P("fact"),
        P(None, "fact"),
        P(("groups", "scen"), None),
    )
    return jax.shard_map(
        on_device,
        mesh=mesh,
        in_specs=placed,
        out_specs=(P(("groups", "scen"), "fact"), P(("groups", "fact"))),
        check_vma=False,
    )
```

time: 155 us -> 127 us (0.82)
  starting transfers between devices: 55.1 us -> 24.6 us
  blocking collectives: 77.5 us -> 60.2 us
  Pallas kernels: 0 us -> 10.5 us
  waiting for transfers between devices: 9.5 us -> 16.9 us
  matrix products: 2.15 us -> 0 us
  other arithmetic: 3.08 us -> 5.16 us
    all_gather x1 -> x0, blocking collectives: 58.5 us -> none  [total_of_pieces(): return lax.all_gather(x, axis).sum(0)]
    all_to_all x5 -> x1, blocking collectives: 19 us -> 60.2 us  [exchange(): lax.all_to_all(pieces, axes, 0, 0, tiled=True, axis_index_groups=groups)]
    all_to_all x2, starting transfers between devices: 49 us -> 16.5 us  [exchange(): lax.all_to_all(pieces, axes, 0, 0, tiled=True, axis_index_groups=groups)]
    pallas_call x0 -> x4, Pallas kernels: none -> 10.5 us  [call(): pl.pallas_call(body, out_shape=out_shape, in_specs=[pl.BlockSpec(memory_s...]
    all_to_all x2, waiting for transfers between devices: 5.21 us -> 13 us  [exchange(): lax.all_to_all(pieces, axes, 0, 0, tiled=True, axis_index_groups=groups)]
    broadcast_in_dim x0 -> x3, other arithmetic: none -> 2.29 us  [the longest x1 0.84 us: reduce_over_trades(): jnp.broadcast_to(pieces[:, None, None], (NEAR, cols, 1, length))]
    dot_general x9 -> x0, matrix products: 2.15 us -> none  [the longest x1 0.3 us: initial_margin_reverse(): jnp.einsum('nsk,kb->nsb', weighted_bar * factor_risk_weight * netted_sens...]
    ppermute x0 -> x1, starting transfers between devices: none -> 1.94 us  [on_device(): other = lax.ppermute(mine, 'fact', [(0, 1), (1, 0)])]
  transfers between devices with their start and end apart: 4 -> 5, of which waited for: 2 -> 3; matrix products, arithmetic and copies ran while one was open for 1% -> 2% of each run, Pallas kernels for 0% -> 1%
where the time goes in v1:
time: 127 us; the launch traced here: 126 us
  blocking collectives  60.2 us (47%)
  starting transfers between devices  24.6 us (19%)
  waiting for transfers between devices  16.9 us (13%)
  Pallas kernels  10.5 us (8%)
  local copies, waits for them, and re-layouts  7.77 us (6%)
  other arithmetic  5.16 us (4%)
    all_to_all x1, blocking collectives, exchange(): lax.all_to_all(pieces, axes, 0, 0, tiled=True, axis_index_groups=groups)  60.2 us
    all_to_all x2, starting transfers between devices, exchange(): lax.all_to_all(pieces, axes, 0, 0, tiled=True, axis_index_groups=groups)  16.5 us
    all_to_all x2, waiting for transfers between devices, exchange(): lax.all_to_all(pieces, axes, 0, 0, tiled=True, axis_index_groups=groups)  13 us
    pallas_call x4, Pallas kernels, call(): pl.pallas_call(body, out_shape=out_shape, in_specs=[pl.BlockSpec(memory_s...  10.5 us
    ppermute x2, starting transfers between devices, shifted(): return lax.ppermute(x, axis, pairs)  6.14 us
    unnamed x21, local copies, waits for them, and re-layouts  4.28 us
    ppermute x2, waiting for transfers between devices, shifted(): return lax.ppermute(x, axis, pairs)  3.94 us
  transfers between devices with their start and end apart: 5, of which 3 were waited for; matrix products, arithmetic and copies ran while one was open for 2% of the time, Pallas kernels for 1%

profile of v1, /device:TPU:40, one launch (start us, length us, event | category | flops | bytes accessed | tf_op | source)
XLA Modules:
  0.0 125.9 jit_solution(2174035503611529979)
XLA Ops:
  0.6 0.7 convert_bitcast_fusion.1
  1.3 0.7 copy-done.5
  2.6 1.8 %shard_map.114.mine = bf16[1432,128]{1,0:T(8,128)(2,1)} custom-call(bf16[512,128]{1,0:T(8,128)(2,1)} %load.1, bf16[512,128]{1,0:T(8,128)(2,1)} %curve.1, f32[256,128]{1,0:T(8,128)} %corr.3, f32[8,128]{1,0:T(8,128)} %copy-done.4), custom_call_target="tpu_custom_call" | custom-call | tf_op jit(solution)/shard_map/pallas_call | solution.py:142
  4.4 1.9 %collective-permute-start = (bf16[1432,128]{1,0:T(8,128)(2,1)}, bf16[1432,128]{1,0:T(8,128)(2,1)S(1)}, u32[]{:S(2)}, u32[]{:S(2)}) collective-permute-start(bf16[1432,128]{1,0:T(8,128)(2,1)} %shard_map.114.mine), channel_id=1, source_target_pairs={{0,1},{1,0},{2,3},{3,2},{4,5},{5,4},{6,7},{7,6},{8,9},{9,8},{10,11... | collective-permute-start | bytes 1099784 | tf_op jit(solution)/shard_map/ppermute | solution.py:215
  6.3 1.8 %shard_map.113 = (f32[32,512]{1,0:T(8,128)}, bf16[32,1024]{1,0:T(8,128)(2,1)}) custom-call(bf16[32,256]{1,0:T(8,128)(2,1)} %state.1, bf16[512,256]{1,0:T(8,128)(2,1)} %direction.3), custom_call_target="tpu_custom_call" | custom-call | tf_op jit(solution)/shard_map/pallas_call | solution.py:142
  8.2 0.7 copy-done
  9.0 2.3 %shard_map.115.net = f32[160,256]{1,0:T(8,128)} custom-call(bf16[32,1024]{1,0:T(8,128)(2,1)} %get-tuple-element.30.pair, s32[1,512]{1,0:T(1,128)} %bitcast.18, bf16[1432,128]{1,0:T(8,128)(2,1)} %shard_map.114.mine, bf16[1432,128]{1,0:T(8,128)(2,1)} %copy-done), custom_call_target="tpu_custom_call" | custom-call | tf_op jit(solution)/shard_map/pallas_call | solution.py:142
  11.3 0.8 fusion.2
  12.1 4.8 %collective-permute-start.1 = (f32[32,256]{1,0:T(8,128)S(1)}, f32[32,256]{1,0:T(8,128)S(1)}, u32[]{:S(2)}, u32[]{:S(2)}) collective-permute-start(f32[32,256]{1,0:T(8,128)S(1)} %get-tuple-element.35), channel_id=1, source_target_pairs={{0,8},{8,16},{16,24},{24,32},{32,40},{40,48},{48,56},{56,64},{64,7... | collective-permute-start | bytes 98312 | tf_op jit(solution)/shard_map/ppermute | solution.py:153
  16.9 1.3 %collective-permute-start.2 = (f32[32,256]{1,0:T(8,128)S(1)}, f32[32,256]{1,0:T(8,128)S(1)}, u32[]{:S(2)}, u32[]{:S(2)}) collective-permute-start(f32[32,256]{1,0:T(8,128)S(1)} %get-tuple-element.34), channel_id=1, source_target_pairs={{8,0},{16,8},{24,16},{32,24},{40,32},{48,40},{56,48},{64,56},{72,6... | collective-permute-start | bytes 98312 | tf_op jit(solution)/shard_map/ppermute | solution.py:153
  18.8 0.8 reshape.131.fund
  19.6 3.9 %collective-permute-done.2.below = f32[32,256]{1,0:T(8,128)S(1)} collective-permute-done((f32[32,256]{1,0:T(8,128)S(1)}, f32[32,256]{1,0:T(8,128)S(1)}, u32[]{:S(2)}, u32[]{:S(2)}) %collective-permute-start.2) | collective-permute-done | bytes 32800 | tf_op jit(solution)/shard_map/ppermute | solution.py:153
  24.1 4.5 %shard_map.116 = (f32[32,128]{1,0:T(8,128)}, f32[8,128]{1,0:T(8,128)}) custom-call(f32[160,256]{1,0:T(8,128)} %shard_map.115.net, f32[32,256]{1,0:T(8,128)} %copy-done.2, f32[32,256]{1,0:T(8,128)} %copy-done.3, f32[32,512]{1,0:T(8,128)} %get-tuple-element.31.money, s32[1,512]{1,0:T(1,128)} %bitcast.19, bf16[1432,128]{1,0:T(8,128)(2,1)} %shard_map.114.mine, ...), custom_call_target="tpu_custom_call" | custom-call | tf_op jit(solution)/shard_map/pallas_call | solution.py:142
  28.7 0.7 convert.19
  29.4 0.7 convert_bitcast_fusion
  30.7 0.8 reduce.7
  31.5 0.7 reshape.134
  32.2 13.2 %all-to-all-start = ((bf16[16,2,576]{2,1,0:T(2,128)(2,1)}), bf16[16,2,576]{2,1,0:T(2,128)(2,1)S(1)}, u32[]{:S(2)}, u32[]{:S(2)}) async-start(bf16[16,2,576]{2,1,0:T(2,128)(2,1)} %reshape.134), calls=%async_computation | async-start | bytes 81920 | tf_op jit(solution)/shard_map/all_to_all | solution.py:157
  45.5 8.0 %all-to-all-done = bf16[16,2,576]{2,1,0:T(2,128)(2,1)S(1)} async-done(((bf16[16,2,576]{2,1,0:T(2,128)(2,1)}), bf16[16,2,576]{2,1,0:T(2,128)(2,1)S(1)}, u32[]{:S(2)}, u32[]{:S(2)}) %all-to-all-start) | async-done | bytes 36896 | tf_op jit(solution)/shard_map/all_to_all | solution.py:157
  53.9 0.7 reduce.8
  54.8 60.2 %all_to_all.15 = bf16[8,2,576]{2,1,0:T(2,128)(2,1)S(1)} all-to-all(bf16[8,2,576]{2,1,0:T(2,128)(2,1)S(1)} %reshape.136), channel_id=1, replica_groups={{0,32,64,96,128,160,192,224},{8,40,72,104,136,168,200,232},{16,48,80,11..., dimensions={0} | all-to-all | bytes 36864 | tf_op jit(solution)/shard_map/all_to_all | solution.py:157
  115.1 0.7 reduce.9
  116.4 3.3 %all-to-all-start.2 = ((bf16[4,2,512]{2,1,0:T(2,128)(2,1)}), bf16[4,2,512]{2,1,0:T(2,128)(2,1)S(1)}, u32[]{:S(2)}, u32[]{:S(2)}) async-start(bf16[4,2,512]{2,1,0:T(2,128)(2,1)} %reshape.138), calls=%async_computation.2 | async-start | bytes 16384 | tf_op jit(solution)/shard_map/all_to_all | solution.py:157
  120.3 5.0 %all-to-all-done.2 = bf16[4,2,512]{2,1,0:T(2,128)(2,1)S(1)} async-done(((bf16[4,2,512]{2,1,0:T(2,128)(2,1)}), bf16[4,2,512]{2,1,0:T(2,128)(2,1)S(1)}, u32[]{:S(2)}, u32[]{:S(2)}) %all-to-all-start.2) | async-done | bytes 8224 | tf_op jit(solution)/shard_map/all_to_all | solution.py:157
  (43 shorter events, 4.9 us)
Async XLA Ops:
  1.3 0.7 copy-start.5
  2.0 0.6 copy-start.4
  4.4 3.9 %collective-permute-start = (bf16[1432,128]{1,0:T(8,128)(2,1)}, bf16[1432,128]{1,0:T(8,128)(2,1)S(1)}, u32[]{:S(2)}, u32[]{:S(2)}) collective-permute-start(bf16[1432,128]{1,0:T(8,128)(2,1)} %shard_map.114.mine), channel_id=1, source_target_pairs={{0,1},{1,0},{2,3},{3,2},{4,5},{5,4},{6,7},{7,6},{8,9},{9,8},{10,11... | collective-permute-start | bytes 1099784 | tf_op jit(solution)/shard_map/ppermute | solution.py:215
  6.3 1.8 %copy-start.1 = (f32[32,128]{1,0:T(8,128)S(1)}, f32[32,128]{1,0:T(8,128)}, u32[]{:S(2)}) copy-start(f32[32,128]{1,0:T(8,128)} %param.23) | copy-start | bytes 49156
  8.2 0.7 copy-start
  12.1 6.2 %copy-start.6 = (f32[12]{0:T(128)S(1)}, f32[12]{0:T(128)}, u32[]{:S(2)}) copy-start(f32[12]{0:T(128)} %param.20) | copy-start | bytes 148
  12.1 7.5 %collective-permute-start.1 = (f32[32,256]{1,0:T(8,128)S(1)}, f32[32,256]{1,0:T(8,128)S(1)}, u32[]{:S(2)}, u32[]{:S(2)}) collective-permute-start(f32[32,256]{1,0:T(8,128)S(1)} %get-tuple-element.35), channel_id=1, source_target_pairs={{0,8},{8,16},{16,24},{24,32},{32,40},{40,48},{48,56},{56,64},{64,7... | collective-permute-start | bytes 98312 | tf_op jit(solution)/shard_map/ppermute | solution.py:153
  16.9 6.6 %collective-permute-start.2 = (f32[32,256]{1,0:T(8,128)S(1)}, f32[32,256]{1,0:T(8,128)S(1)}, u32[]{:S(2)}, u32[]{:S(2)}) collective-permute-start(f32[32,256]{1,0:T(8,128)S(1)} %get-tuple-element.34), channel_id=1, source_target_pairs={{8,0},{16,8},{24,16},{32,24},{40,32},{48,40},{56,48},{64,56},{72,6... | collective-permute-start | bytes 98312 | tf_op jit(solution)/shard_map/ppermute | solution.py:153
  19.6 3.9 %copy-start.2 = (f32[32,256]{1,0:T(8,128)}, f32[32,256]{1,0:T(8,128)S(1)}, u32[]{:S(2)}) copy-start(f32[32,256]{1,0:T(8,128)S(1)} %collective-permute-done.1.above) | copy-start | bytes 98308
  23.5 0.6 copy-start.3
  32.2 21.2 %all-to-all-start = ((bf16[16,2,576]{2,1,0:T(2,128)(2,1)}), bf16[16,2,576]{2,1,0:T(2,128)(2,1)S(1)}, u32[]{:S(2)}, u32[]{:S(2)}) async-start(bf16[16,2,576]{2,1,0:T(2,128)(2,1)} %reshape.134), calls=%async_computation | async-start | bytes 81920 | tf_op jit(solution)/shard_map/all_to_all | solution.py:157
  116.4 8.9 %all-to-all-start.2 = ((bf16[4,2,512]{2,1,0:T(2,128)(2,1)}), bf16[4,2,512]{2,1,0:T(2,128)(2,1)S(1)}, u32[]{:S(2)}, u32[]{:S(2)}) async-start(bf16[4,2,512]{2,1,0:T(2,128)(2,1)} %reshape.138), calls=%async_computation.2 | async-start | bytes 16384 | tf_op jit(solution)/shard_map/all_to_all | solution.py:157

commit v2 on v1

v2 whole, which is shorter than its diff:
```python
import jax
import jax.numpy as jnp
from jax import lax
from jax.experimental import pallas as pl
from jax.experimental.pallas import tpu as pltpu
from jax.sharding import PartitionSpec as P

NSET_DEV = 4
SPAN = NSET_DEV + 1
NEAR = 4
F32 = jnp.float32
BF16 = jnp.bfloat16
PRECISE = lax.Precision.HIGHEST


def three_parts(x):
    high = x.astype(BF16)
    rest = x - high.astype(F32)
    mid = rest.astype(BF16)
    low = (rest - mid.astype(F32)).astype(BF16)
    return high, mid, low


def from_parts(high, mid, low):
    return high.astype(F32) + mid.astype(F32) + low.astype(F32)


def dot_t(a, b, **kw):
    return lax.dot_general(a, b, (((1,), (1,)), ((), ())), preferred_element_type=F32, **kw)


def dot(a, b, **kw):
    return lax.dot_general(a, b, (((1,), (0,)), ((), ())), preferred_element_type=F32, **kw)


def pack_kernel(load, curve, corr, risk, bucket, out):
    trades, half = load.shape
    start = pl.multiple_of(lax.axis_index("fact") * half, half)
    out[:trades] = load[...]
    out[trades : 2 * trades] = curve[...]
    for i, part in enumerate(three_parts(corr[pl.ds(start, half)])):
        out[2 * trades + i * half : 2 * trades + (i + 1) * half] = part
    base = 2 * trades + 3 * half
    high, mid, low = three_parts(risk[...])
    for i, row in enumerate((high, mid, low, bucket[...].astype(F32).astype(BF16))):
        out[base + 8 * i : base + 8 * (i + 1)] = jnp.broadcast_to(row, (8, half))


def money_kernel(
    state, direction, corr, sets, funding, threshold,
    money_out, pair_out, side_out, corr_out, where_out, fund_out, limit_out,
):
    money = dot_t(state[...], direction[...])
    money_out[...] = money
    trades, factors = direction.shape
    half = factors // 2
    pair_out[:, :trades] = lax.logistic(money).astype(BF16)
    pair_out[:, trades:] = money.astype(BF16)
    side = pl.multiple_of(lax.axis_index("fact") * half, half)
    side_out[...] = direction[:, pl.ds(side, half)]
    corr_out[...] = corr[...]
    first = lax.axis_index("trades") * NSET_DEV - 1
    place = jnp.broadcast_to(sets[...] - first, (8, trades))
    where_out[:, :trades] = place
    where_out[:, trades:] = place
    fund_out[...] = funding[...]
    buckets = lax.broadcasted_iota(jnp.int32, limit_out.shape, 1)
    limit = jnp.ones(limit_out.shape, F32)
    for i in range(threshold.shape[0]):
        limit = jnp.where(buckets == i, threshold[i], limit)
    limit_out[...] = limit


def window_kernel(pair, where, mine, other, low_out, mid_out, high_out):
    scen, double = pair.shape
    paired = pair[...]
    place = where[:1]
    half = mine.shape[1]
    for w in range(SPAN):
        member = jnp.where(place == w, 1.0, 0.0).astype(BF16)
        mixing = paired * member
        if w == 0:
            out, at = low_out, 0
        elif w < SPAN - 1:
            out, at = mid_out, (w - 1) * scen
        else:
            out, at = high_out, 0
        out[at : at + scen, :half] = dot(mixing, mine[:double])
        out[at : at + scen, half:] = dot(mixing, other[:double])


def sets_kernel(
    low, mid, high, above, below, mine, other, corr, fund, limits, bar_out, weight_out
):
    scen, factors = low.shape
    half = factors // 2
    double = mine.shape[0] - 3 * half - 32
    side = pl.multiple_of(lax.axis_index("fact") * half, half)
    far_side = pl.multiple_of((1 - lax.axis_index("fact")) * half, half)
    netted = jnp.concatenate([low[...] + above[...], mid[...], high[...] + below[...]], axis=0)
    base = double + 3 * half

    def risk_of(ref):
        return from_parts(ref[base : base + 1], ref[base + 8 : base + 9], ref[base + 16 : base + 17])

    def bucket_of(ref):
        return ref[base + 24 : base + 25].astype(F32)

    risk = jnp.concatenate([risk_of(mine), risk_of(other)], axis=1)
    bucket = jnp.concatenate([bucket_of(mine), bucket_of(other)], axis=1).astype(jnp.int32)
    hot = jnp.where(
        lax.broadcasted_iota(jnp.int32, (16, factors), 0) == bucket, 1.0, 0.0
    ).astype(F32)
    limit = limits[:1, :16]
    bucket_sum = dot_t(netted, hot, precision=PRECISE)
    raw_ratio = jnp.sqrt(jnp.abs(bucket_sum) / limit)
    concentration = jnp.maximum(1.0, raw_ratio)
    conc_factor = dot(concentration, hot, precision=PRECISE)
    scaled = risk * conc_factor
    weighted = scaled * netted
    near_cols = corr[pl.ds(side, half)]
    cross = corr[pl.ds(far_side, half)]
    far_cols = from_parts(*[other[double + i * half : double + (i + 1) * half] for i in range(3)])
    w_own, w_far = weighted[:, :half], weighted[:, half:]
    image = jnp.concatenate(
        [
            dot(w_own, near_cols, precision=PRECISE) + dot(w_far, cross, precision=PRECISE),
            dot_t(w_own, cross, precision=PRECISE) + dot(w_far, far_cols, precision=PRECISE),
        ],
        axis=1,
    )
    margin = jnp.sqrt(jnp.sum(weighted * image, axis=1, keepdims=True) + 1e-06)
    first = lax.axis_index("trades") * NSET_DEV - 1
    costs = fund[...]
    lanes = lax.broadcasted_iota(jnp.int32, costs.shape, 1)
    cost = jnp.concatenate(
        [
            jnp.sum(jnp.where(lanes == first + w, costs, 0.0), axis=1, keepdims=True)
            for w in range(SPAN)
        ],
        axis=0,
    )
    weighted_bar = (cost / margin) * image
    conc_bar = dot_t(weighted_bar * risk * netted, hot, precision=PRECISE)
    sign = jnp.where(bucket_sum > 0.0, 1.0, jnp.where(bucket_sum < 0.0, -1.0, 0.0))
    bucket_bar = jnp.where(raw_ratio > 1.0, conc_bar * sign / (2.0 * limit * concentration), 0.0)
    bar_out[...] = (weighted_bar * scaled + dot(bucket_bar, hot, precision=PRECISE)).astype(BF16)
    grad = weighted_bar[scen:, :half] * netted[scen:, :half] * conc_factor[scen:, :half]
    weight_out[...] = jnp.broadcast_to(jnp.sum(grad, axis=0, keepdims=True), weight_out.shape)


def pull_kernel(bar, mine, other, where, money, side, state_out):
    scen, trades = money.shape
    double = 2 * trades
    half = side.shape[1]
    place = where[:1]
    spread = dot_t(bar[:, :half], mine[:double]) + dot_t(bar[:, half:], other[:double])
    pulled = jnp.zeros((scen, double), F32)
    for w in range(SPAN):
        pulled = pulled + jnp.where(place == w, spread[w * scen : (w + 1) * scen], 0.0)
    likely = lax.logistic(money[...])
    money_bar = (pulled[:, :trades] * likely * (1.0 - likely) + pulled[:, trades:]).astype(BF16)
    state_out[...] = dot(money_bar, side[...]).astype(BF16)


def near_vmem(x):
    return pltpu.with_memory_space_constraint(x, pltpu.VMEM)


def call(body, out_shape, *args, smem=()):
    return pl.pallas_call(
        body,
        out_shape=out_shape,
        in_specs=[
            pl.BlockSpec(memory_space=pltpu.SMEM if i in smem else pltpu.VMEM)
            for i in range(len(args))
        ],
        out_specs=jax.tree.map(lambda _: pl.BlockSpec(memory_space=pltpu.VMEM), out_shape),
    )(*args)


def shifted(x, axis, by):
    size = lax.axis_size(axis)
    pairs = [(i, i + by) for i in range(size) if 0 <= i + by < size]
    return lax.ppermute(x, axis, pairs)


def sum_over_trades(part):
    devs = lax.axis_size("trades")
    blocks = devs // NEAR
    place = lambda b, j: (b * NEAR + j - NEAR // 2) % devs
    mine = ((lax.axis_index("trades") + NEAR // 2) % devs) // NEAR
    groups = [[place(b, j) for j in range(NEAR)] for b in range(blocks)]
    copies = jnp.broadcast_to(part[None], (NEAR, *part.shape))
    got = lax.all_to_all(copies, "trades", 0, 0, tiled=True, axis_index_groups=groups)
    total = jnp.sum(got.astype(F32), axis=0)

    def send(x, *links):
        pairs = [(place(a, j), place(b, j)) for a, b in links for j in range(NEAR)]
        return lax.ppermute(x, "trades", pairs)

    def add(x, *links):
        return x + send(x.astype(BF16), *links).astype(F32)

    total = add(total, (4, 3), (2, 1))
    total = add(total, (5, 3), (6, 7))
    total = add(total, (3, 1))
    out = total.astype(BF16)
    whole = (total + send(out, (7, 0)).astype(F32) + send(out, (1, 0)).astype(F32)).astype(BF16)
    first = send(whole, (0, 1))
    second = send(whole, (0, 2))
    third = send(whole, (0, 3))
    first, second, third = lax.optimization_barrier((first, second, third))
    fourth = send(jnp.where(mine == 3, third, second), (3, 4), (2, 7))
    fifth = send(fourth, (4, 5), (7, 6))
    return jnp.where(mine == 0, whole, first + second + third + fourth + fifth)


def on_device(
    scenario_state,
    direction,
    trade_load,
    trade_curve,
    trade_set,
    factor_bucket_index,
    threshold,
    factor_risk_weight,
    correlation,
    funding,
):
    scen, set_count = funding.shape
    trades, half = trade_load.shape
    double, factors = 2 * trades, 2 * half
    mine = call(
        pack_kernel,
        pltpu.VMEM((double + 3 * half + 32, half), BF16),
        trade_load, trade_curve, correlation,
        factor_risk_weight.reshape(1, half), factor_bucket_index.reshape(1, half),
    )
    other = lax.ppermute(mine, "fact", [(0, 1), (1, 0)])
    money, pair, side, corr, where, fund, limit = call(
        money_kernel,
        (
            pltpu.VMEM((scen, trades), F32),
            pltpu.VMEM((scen, double), BF16),
            pltpu.VMEM((trades, half), BF16),
            pltpu.VMEM((factors, half), F32),
            pltpu.VMEM((8, double), jnp.int32),
            pltpu.VMEM(funding.shape, F32),
            pltpu.VMEM((8, 128), F32),
        ),
        near_vmem(scenario_state), near_vmem(direction), near_vmem(correlation),
        near_vmem(trade_set.reshape(1, trades)), near_vmem(funding), threshold,
        smem=(5,),
    )
    mine, other = near_vmem(mine), near_vmem(other)
    money, pair, side, corr, where, fund, limit = map(
        near_vmem, (money, pair, side, corr, where, fund, limit)
    )
    low, mid, high = call(
        window_kernel,
        (
            pltpu.VMEM((scen, factors), F32),
            pltpu.VMEM(((SPAN - 2) * scen, factors), F32),
            pltpu.VMEM((scen, factors), F32),
        ),
        pair, where, mine, other,
    )
    below = near_vmem(shifted(low, "trades", -1))
    above = near_vmem(shifted(high, "trades", 1))
    low, mid, high = near_vmem(low), near_vmem(mid), near_vmem(high)
    bar, weight = call(
        sets_kernel,
        (pltpu.VMEM((SPAN * scen, factors), BF16), pltpu.VMEM((8, half), F32)),
        low, mid, high, above, below, mine, other, corr, fund, limit,
    )
    for step in (1, 2):
        pairs = [(i, i ^ step) for i in range(lax.axis_size("scen"))]
        weight = weight + lax.ppermute(weight, "scen", pairs)
    state_part = call(
        pull_kernel,
        pltpu.VMEM((scen, half), BF16),
        near_vmem(bar), mine, other, where, money, side,
    )
    total = sum_over_trades(jnp.concatenate([state_part, weight.astype(BF16)], axis=0)).astype(F32)
    weight_grad = total[scen] / (scen * lax.axis_size("scen") * set_count)
    return (total[:scen], weight_grad)


def solution(mesh):
    placed = (
        P(("groups", "scen"), None),
        P("trades", None),
        P("trades", "fact"),
        P("trades", "fact"),
        P("trades"),
        P("fact"),
        P(),
        P("fact"),
        P(None, "fact"),
        P(("groups", "scen"), None),
    )
    return jax.shard_map(
        on_device,
        mesh=mesh,
        in_specs=placed,
        out_specs=(P(("groups", "scen"), "fact"), P(("groups", "fact"))),
        check_vma=False,
    )
```

time: 127 us -> 114 us (0.90)
  waiting for transfers between devices: 16.9 us -> 32.3 us
  blocking collectives: 60.2 us -> 47.1 us
  local copies, waits for them, and re-layouts: 7.77 us -> 0.64 us
  Pallas kernels: 10.5 us -> 4.97 us
  other arithmetic: 5.16 us -> 0.6 us
  starting transfers between devices: 24.6 us -> 26.9 us
    ppermute x0 -> x12, waiting for transfers between devices: none -> 26.3 us  [the longest x10 23 us: send(): return lax.ppermute(x, 'trades', pairs)]
    ppermute x0 -> x12, starting transfers between devices: none -> 19 us  [the longest x10 10.2 us: send(): return lax.ppermute(x, 'trades', pairs)]
    all_to_all x2 -> x0, starting transfers between devices: 16.5 us -> none  [exchange(): lax.all_to_all(pieces, axes, 0, 0, tiled=True, axis_index_groups=groups)]
    all_to_all x1, blocking collectives: 60.2 us -> 47.1 us  [sum_over_trades(): lax.all_to_all(copies, 'trades', 0, 0, tiled=True, axis_index_groups=groups)]
    all_to_all x2 -> x0, waiting for transfers between devices: 13 us -> none  [exchange(): lax.all_to_all(pieces, axes, 0, 0, tiled=True, axis_index_groups=groups)]
    pallas_call x4 -> x5, Pallas kernels: 10.5 us -> 4.97 us  [call(): pl.pallas_call(body, out_shape=out_shape, in_specs=[pl.BlockSpec(memory_s...]
    unnamed x21 -> x10, local copies, waits for them, and re-layouts: 4.28 us -> 0.02 us
    broadcast_in_dim x3 -> x0, other arithmetic: 2.29 us -> none  [the longest x1 0.84 us: reduce_over_trades(): jnp.broadcast_to(pieces[:, None, None], (NEAR, cols, 1, length))]
  transfers between devices with their start and end apart: 5 -> 15, of which waited for: 3 -> 7; matrix products, arithmetic and copies ran while one was open for 2% -> 0% of each run, Pallas kernels for 1% -> 1%
where the time goes in v2:
time: 114 us
  blocking collectives  47.1 us (41%)
  waiting for transfers between devices  32.3 us (28%)
  starting transfers between devices  26.9 us (24%)
  Pallas kernels  4.97 us (4%)
    all_to_all x1, blocking collectives, sum_over_trades(): lax.all_to_all(copies, 'trades', 0, 0, tiled=True, axis_index_groups=groups)  47.1 us
    ppermute x10, waiting for transfers between devices, send(): return lax.ppermute(x, 'trades', pairs)  23 us
    ppermute x10, starting transfers between devices, send(): return lax.ppermute(x, 'trades', pairs)  10.2 us
    ppermute x2, starting transfers between devices, on_device(): weight = weight + lax.ppermute(weight, 'scen', pairs)  8.78 us
    ppermute x2, starting transfers between devices, shifted(): return lax.ppermute(x, axis, pairs)  6.02 us
    ppermute x2, waiting for transfers between devices, shifted(): return lax.ppermute(x, axis, pairs)  5.29 us
    pallas_call x5, Pallas kernels, call(): pl.pallas_call(body, out_shape=out_shape, in_specs=[pl.BlockSpec(memory_s...  4.97 us
    ppermute x2, waiting for transfers between devices, on_device(): weight = weight + lax.ppermute(weight, 'scen', pairs)  3.29 us
  transfers between devices with their start and end apart: 15, of which 7 were waited for; matrix products, arithmetic and copies ran while one was open for 0% of the time, Pallas kernels for 1%

profile of v2, /device:TPU:40, one launch (start us, length us, event | category | flops | bytes accessed | tf_op | source)
XLA Modules:
  0.0 113.6 jit_solution(672128972261357445)
XLA Ops:
  0.7 1.1 %shard_map.114.mine = bf16[1440,128]{1,0:T(8,128)(2,1)S(1)} custom-call(bf16[512,128]{1,0:T(8,128)(2,1)} %load.1, bf16[512,128]{1,0:T(8,128)(2,1)} %curve.1, f32[256,128]{1,0:T(8,128)} %corr.3, f32[1,128]{1,0:T(1,128)} %bitcast.6, s32[1,128]{1,0:T(1,128)} %bitcast.7), custom_call_target="tpu_custom_call" | custom-call | tf_op jit(solution)/shard_map/pallas_call | solution.py:171
  1.8 2.0 %collective-permute-start = (bf16[1440,128]{1,0:T(8,128)(2,1)S(1)}, bf16[1440,128]{1,0:T(8,128)(2,1)S(1)}, u32[]{:S(2)}, u32[]{:S(2)}) collective-permute-start(bf16[1440,128]{1,0:T(8,128)(2,1)S(1)} %shard_map.114.mine), channel_id=1, source_target_pairs={{0,1},{1,0},{2,3},{3,2},{4,5},{5,4},{6,7},{7,6},{8,9},{9,8},{10,11... | collective-permute-start | bytes 1105928 | tf_op jit(solution)/shard_map/ppermute | solution.py:240
  3.8 0.9 shard_map.113
  4.7 0.7 collective-permute-done.other
  5.9 4.7 %collective-permute-start.1 = (f32[32,256]{1,0:T(8,128)S(1)}, f32[32,256]{1,0:T(8,128)S(1)}, u32[]{:S(2)}, u32[]{:S(2)}) collective-permute-start(f32[32,256]{1,0:T(8,128)S(1)} %get-tuple-element.21.high), channel_id=1, source_target_pairs={{0,8},{8,16},{16,24},{24,32},{32,40},{40,48},{48,56},{56,64},{64,7... | collective-permute-start | bytes 98312 | tf_op jit(solution)/shard_map/ppermute | solution.py:185
  10.6 1.3 %collective-permute-start.2 = (f32[32,256]{1,0:T(8,128)S(1)}, f32[32,256]{1,0:T(8,128)S(1)}, u32[]{:S(2)}, u32[]{:S(2)}) collective-permute-start(f32[32,256]{1,0:T(8,128)S(1)} %get-tuple-element.19.low), channel_id=1, source_target_pairs={{8,0},{16,8},{24,16},{32,24},{40,32},{48,40},{56,48},{64,56},{72,6... | collective-permute-start | bytes 98312 | tf_op jit(solution)/shard_map/ppermute | solution.py:185
  12.2 5.0 %collective-permute-done.2.below = f32[32,256]{1,0:T(8,128)S(1)} collective-permute-done((f32[32,256]{1,0:T(8,128)S(1)}, f32[32,256]{1,0:T(8,128)S(1)}, u32[]{:S(2)}, u32[]{:S(2)}) %collective-permute-start.2) | collective-permute-done | bytes 32800 | tf_op jit(solution)/shard_map/ppermute | solution.py:185
  17.2 2.0 %shard_map.116 = (bf16[160,256]{1,0:T(8,128)(2,1)S(1)}, f32[8,128]{1,0:T(8,128)S(1)}) custom-call(f32[32,256]{1,0:T(8,128)S(1)} %get-tuple-element.19.low, f32[96,256]{1,0:T(8,128)S(1)} %get-tuple-element.20.mid, f32[32,256]{1,0:T(8,128)S(1)} %get-tuple-element.21.high, f32[32,256]{1,0:T(8,128)S(1)} %collective-permute-done.1.above, ...), custom_call_target="tpu_custom_call" | custom-call | tf_op jit(solution)/shard_map/pallas_call | solution.py:171
  19.3 3.6 %collective-permute-start.3 = (f32[8,128]{1,0:T(8,128)S(1)}, f32[8,128]{1,0:T(8,128)S(1)}, u32[]{:S(2)}, u32[]{:S(2)}) collective-permute-start(f32[8,128]{1,0:T(8,128)S(1)} %get-tuple-element.28), channel_id=1, source_target_pairs={{0,2},{2,0},{4,6},{6,4},{1,3},{3,1},{5,7},{7,5},{8,10},{10,8},{12,... | collective-permute-start | bytes 12296 | tf_op jit(solution)/shard_map/ppermute | solution.py:279
  22.9 2.0 %collective-permute-done.3 = f32[8,128]{1,0:T(8,128)S(1)} collective-permute-done((f32[8,128]{1,0:T(8,128)S(1)}, f32[8,128]{1,0:T(8,128)S(1)}, u32[]{:S(2)}, u32[]{:S(2)}) %collective-permute-start.3) | collective-permute-done | bytes 4128 | tf_op jit(solution)/shard_map/ppermute | solution.py:279
  24.8 5.2 %collective-permute-start.4 = (f32[8,128]{1,0:T(8,128)S(1)}, f32[8,128]{1,0:T(8,128)S(1)}, u32[]{:S(2)}, u32[]{:S(2)}) collective-permute-start(f32[8,128]{1,0:T(8,128)S(1)} %add.43), channel_id=1, source_target_pairs={{0,4},{2,6},{4,0},{6,2},{1,5},{3,7},{5,1},{7,3},{8,12},{10,14},{12... | collective-permute-start | bytes 12296 | tf_op jit(solution)/shard_map/ppermute | solution.py:279
  30.5 1.3 %collective-permute-done.4 = f32[8,128]{1,0:T(8,128)S(1)} collective-permute-done((f32[8,128]{1,0:T(8,128)S(1)}, f32[8,128]{1,0:T(8,128)S(1)}, u32[]{:S(2)}, u32[]{:S(2)}) %collective-permute-start.4) | collective-permute-done | bytes 4128 | tf_op jit(solution)/shard_map/ppermute | solution.py:279
  31.9 47.1 %all_to_all.5 = bf16[4,40,128]{2,1,0:T(8,128)(2,1)S(1)} all-to-all(bf16[4,40,128]{2,1,0:T(8,128)(2,1)S(1)} %broadcast_in_dim.2), channel_id=1, replica_groups={{240,248,0,8},{16,24,32,40},{48,56,64,72},{80,88,96,104},{112,120,128,1..., dimensions={0} | all-to-all | bytes 81920 | tf_op jit(solution)/shard_map/all_to_all | solution.py:195
  79.0 0.7 collective-permute-start.5
  79.7 0.7 collective-permute-start.6
  80.4 0.7 collective-permute-start.7
  81.1 1.3 %collective-permute-start.9 = (bf16[40,128]{1,0:T(8,128)(2,1)S(1)}, bf16[40,128]{1,0:T(8,128)(2,1)S(1)}, u32[]{:S(2)}, u32[]{:S(2)}) collective-permute-start(bf16[40,128]{1,0:T(8,128)(2,1)S(1)} %fusion.1), channel_id=1, source_target_pairs={{16,240},{24,248},{32,0},{40,8},{17,241},{25,249},{33,1},{41,9},{1... | collective-permute-start | bytes 30728 | tf_op jit(solution)/shard_map/ppermute | solution.py:200
  82.4 1.3 %collective-permute-start.8 = (bf16[40,128]{1,0:T(8,128)(2,1)S(1)}, bf16[40,128]{1,0:T(8,128)(2,1)S(1)}, u32[]{:S(2)}, u32[]{:S(2)}) collective-permute-start(bf16[40,128]{1,0:T(8,128)(2,1)S(1)} %fusion.1), channel_id=1, source_target_pairs={{208,240},{216,248},{224,0},{232,8},{209,241},{217,249},{225,1},{2... | collective-permute-start | bytes 30728 | tf_op jit(solution)/shard_map/ppermute | solution.py:200
  83.8 21.6 %collective-permute-done.9 = bf16[40,128]{1,0:T(8,128)(2,1)S(1)} collective-permute-done((bf16[40,128]{1,0:T(8,128)(2,1)S(1)}, bf16[40,128]{1,0:T(8,128)(2,1)S(1)}, u32[]{:S(2)}, u32[]{:S(2)}) %collective-permute-start.9) | collective-permute-done | bytes 10272 | tf_op jit(solution)/shard_map/ppermute | solution.py:200
  105.4 1.7 %collective-permute-start.10 = (bf16[40,128]{1,0:T(8,128)(2,1)S(1)}, bf16[40,128]{1,0:T(8,128)(2,1)S(1)}, u32[]{:S(2)}, u32[]{:S(2)}) collective-permute-start(bf16[40,128]{1,0:T(8,128)(2,1)S(1)} %add_convert_fusion), channel_id=1, source_target_pairs={{240,16},{248,24},{0,32},{8,40},{241,17},{249,25},{1,33},{9,41},{2... | collective-permute-start | bytes 30728 | tf_op jit(solution)/shard_map/ppermute | solution.py:200
  107.1 1.3 %collective-permute-start.11 = (bf16[40,128]{1,0:T(8,128)(2,1)S(1)}, bf16[40,128]{1,0:T(8,128)(2,1)S(1)}, u32[]{:S(2)}, u32[]{:S(2)}) collective-permute-start(bf16[40,128]{1,0:T(8,128)(2,1)S(1)} %add_convert_fusion), channel_id=1, source_target_pairs={{240,48},{248,56},{0,64},{8,72},{241,49},{249,57},{1,65},{9,73},{2... | collective-permute-start | bytes 30728 | tf_op jit(solution)/shard_map/ppermute | solution.py:200
  108.4 1.3 %collective-permute-start.12 = (bf16[40,128]{1,0:T(8,128)(2,1)S(1)}, bf16[40,128]{1,0:T(8,128)(2,1)S(1)}, u32[]{:S(2)}, u32[]{:S(2)}) collective-permute-start(bf16[40,128]{1,0:T(8,128)(2,1)S(1)} %add_convert_fusion), channel_id=1, source_target_pairs={{240,80},{248,88},{0,96},{8,104},{241,81},{249,89},{1,97},{9,105},... | collective-permute-start | bytes 30728 | tf_op jit(solution)/shard_map/ppermute | solution.py:200
  109.8 1.3 %collective-permute-done.12 = bf16[40,128]{1,0:T(8,128)(2,1)S(1)} collective-permute-done((bf16[40,128]{1,0:T(8,128)(2,1)S(1)}, bf16[40,128]{1,0:T(8,128)(2,1)S(1)}, u32[]{:S(2)}, u32[]{:S(2)}) %collective-permute-start.12) | collective-permute-done | bytes 10272 | tf_op jit(solution)/shard_map/ppermute | solution.py:200
  111.8 0.7 collective-permute-start.14
  (36 shorter events, 3.1 us)
Async XLA Ops:
  0.6 3.1 %copy-start = (f32[256,128]{1,0:T(8,128)S(1)}, f32[256,128]{1,0:T(8,128)}, u32[]{:S(2)}) copy-start(f32[256,128]{1,0:T(8,128)} %corr.3) | copy-start | bytes 393220
  0.6 3.1 %copy-start.1 = (bf16[512,256]{1,0:T(8,128)(2,1)S(1)}, bf16[512,256]{1,0:T(8,128)(2,1)}, u32[]{:S(2)}) copy-start(bf16[512,256]{1,0:T(8,128)(2,1)} %direction.1) | copy-start | bytes 786436
  0.7 3.1 %copy-start.2 = (bf16[32,256]{1,0:T(8,128)(2,1)S(1)}, bf16[32,256]{1,0:T(8,128)(2,1)}, u32[]{:S(2)}) copy-start(bf16[32,256]{1,0:T(8,128)(2,1)} %state.1) | copy-start | bytes 49156
  0.7 3.1 %copy-start.3 = (f32[32,128]{1,0:T(8,128)S(1)}, f32[32,128]{1,0:T(8,128)}, u32[]{:S(2)}) copy-start(f32[32,128]{1,0:T(8,128)} %funding.1) | copy-start | bytes 49156
  0.7 3.1 %copy-start.4 = (s32[512]{0:T(512)S(1)}, s32[512]{0:T(512)}, u32[]{:S(2)}) copy-start(s32[512]{0:T(512)} %param.14) | copy-start | bytes 6148
  1.8 3.6 %collective-permute-start = (bf16[1440,128]{1,0:T(8,128)(2,1)S(1)}, bf16[1440,128]{1,0:T(8,128)(2,1)S(1)}, u32[]{:S(2)}, u32[]{:S(2)}) collective-permute-start(bf16[1440,128]{1,0:T(8,128)(2,1)S(1)} %shard_map.114.mine), channel_id=1, source_target_pairs={{0,1},{1,0},{2,3},{3,2},{4,5},{5,4},{6,7},{7,6},{8,9},{9,8},{10,11... | collective-permute-start | bytes 1105928 | tf_op jit(solution)/shard_map/ppermute | solution.py:240
  5.9 6.3 %collective-permute-start.1 = (f32[32,256]{1,0:T(8,128)S(1)}, f32[32,256]{1,0:T(8,128)S(1)}, u32[]{:S(2)}, u32[]{:S(2)}) collective-permute-start(f32[32,256]{1,0:T(8,128)S(1)} %get-tuple-element.21.high), channel_id=1, source_target_pairs={{0,8},{8,16},{16,24},{24,32},{32,40},{40,48},{48,56},{56,64},{64,7... | collective-permute-start | bytes 98312 | tf_op jit(solution)/shard_map/ppermute | solution.py:185
  10.6 6.6 %collective-permute-start.2 = (f32[32,256]{1,0:T(8,128)S(1)}, f32[32,256]{1,0:T(8,128)S(1)}, u32[]{:S(2)}, u32[]{:S(2)}) collective-permute-start(f32[32,256]{1,0:T(8,128)S(1)} %get-tuple-element.19.low), channel_id=1, source_target_pairs={{8,0},{16,8},{24,16},{32,24},{40,32},{48,40},{56,48},{64,56},{72,6... | collective-permute-start | bytes 98312 | tf_op jit(solution)/shard_map/ppermute | solution.py:185
  19.3 5.5 %collective-permute-start.3 = (f32[8,128]{1,0:T(8,128)S(1)}, f32[8,128]{1,0:T(8,128)S(1)}, u32[]{:S(2)}, u32[]{:S(2)}) collective-permute-start(f32[8,128]{1,0:T(8,128)S(1)} %get-tuple-element.28), channel_id=1, source_target_pairs={{0,2},{2,0},{4,6},{6,4},{1,3},{3,1},{5,7},{7,5},{8,10},{10,8},{12,... | collective-permute-start | bytes 12296 | tf_op jit(solution)/shard_map/ppermute | solution.py:279
  24.8 7.0 %collective-permute-start.4 = (f32[8,128]{1,0:T(8,128)S(1)}, f32[8,128]{1,0:T(8,128)S(1)}, u32[]{:S(2)}, u32[]{:S(2)}) collective-permute-start(f32[8,128]{1,0:T(8,128)S(1)} %add.43), channel_id=1, source_target_pairs={{0,4},{2,6},{4,0},{6,2},{1,5},{3,7},{5,1},{7,3},{8,12},{10,14},{12... | collective-permute-start | bytes 12296 | tf_op jit(solution)/shard_map/ppermute | solution.py:279
  79.0 0.7 collective-permute-start.5
  79.7 0.7 collective-permute-start.6
  80.4 0.7 collective-permute-start.7
  81.1 24.3 %collective-permute-start.9 = (bf16[40,128]{1,0:T(8,128)(2,1)S(1)}, bf16[40,128]{1,0:T(8,128)(2,1)S(1)}, u32[]{:S(2)}, u32[]{:S(2)}) collective-permute-start(bf16[40,128]{1,0:T(8,128)(2,1)S(1)} %fusion.1), channel_id=1, source_target_pairs={{16,240},{24,248},{32,0},{40,8},{17,241},{25,249},{33,1},{41,9},{1... | collective-permute-start | bytes 30728 | tf_op jit(solution)/shard_map/ppermute | solution.py:200
  82.4 22.9 %collective-permute-start.8 = (bf16[40,128]{1,0:T(8,128)(2,1)S(1)}, bf16[40,128]{1,0:T(8,128)(2,1)S(1)}, u32[]{:S(2)}, u32[]{:S(2)}) collective-permute-start(bf16[40,128]{1,0:T(8,128)(2,1)S(1)} %fusion.1), channel_id=1, source_target_pairs={{208,240},{216,248},{224,0},{232,8},{209,241},{217,249},{225,1},{2... | collective-permute-start | bytes 30728 | tf_op jit(solution)/shard_map/ppermute | solution.py:200
  105.4 4.3 %collective-permute-start.10 = (bf16[40,128]{1,0:T(8,128)(2,1)S(1)}, bf16[40,128]{1,0:T(8,128)(2,1)S(1)}, u32[]{:S(2)}, u32[]{:S(2)}) collective-permute-start(bf16[40,128]{1,0:T(8,128)(2,1)S(1)} %add_convert_fusion), channel_id=1, source_target_pairs={{240,16},{248,24},{0,32},{8,40},{241,17},{249,25},{1,33},{9,41},{2... | collective-permute-start | bytes 30728 | tf_op jit(solution)/shard_map/ppermute | solution.py:200
  107.1 2.7 %collective-permute-start.11 = (bf16[40,128]{1,0:T(8,128)(2,1)S(1)}, bf16[40,128]{1,0:T(8,128)(2,1)S(1)}, u32[]{:S(2)}, u32[]{:S(2)}) collective-permute-start(bf16[40,128]{1,0:T(8,128)(2,1)S(1)} %add_convert_fusion), channel_id=1, source_target_pairs={{240,48},{248,56},{0,64},{8,72},{241,49},{249,57},{1,65},{9,73},{2... | collective-permute-start | bytes 30728 | tf_op jit(solution)/shard_map/ppermute | solution.py:200
  108.4 2.7 %collective-permute-start.12 = (bf16[40,128]{1,0:T(8,128)(2,1)S(1)}, bf16[40,128]{1,0:T(8,128)(2,1)S(1)}, u32[]{:S(2)}, u32[]{:S(2)}) collective-permute-start(bf16[40,128]{1,0:T(8,128)(2,1)S(1)} %add_convert_fusion), channel_id=1, source_target_pairs={{240,80},{248,88},{0,96},{8,104},{241,81},{249,89},{1,97},{9,105},... | collective-permute-start | bytes 30728 | tf_op jit(solution)/shard_map/ppermute | solution.py:200
  111.1 0.7 collective-permute-start.13
  111.8 0.7 collective-permute-start.14

commit v3 on v2

--- a/solution.py
+++ b/solution.py
@@ -90,7 +90,7 @@
 
 
 def sets_kernel(
-    low, mid, high, above, below, mine, other, corr, fund, limits, bar_out, weight_out
+    low, mid, high, above, below, mine, other, corr, fund, limits, where, money, side_of, out
 ):
     scen, factors = low.shape
     half = factors // 2
@@ -144,15 +144,10 @@
     conc_bar = dot_t(weighted_bar * risk * netted, hot, precision=PRECISE)
     sign = jnp.where(bucket_sum > 0.0, 1.0, jnp.where(bucket_sum < 0.0, -1.0, 0.0))
     bucket_bar = jnp.where(raw_ratio > 1.0, conc_bar * sign / (2.0 * limit * concentration), 0.0)
-    bar_out[...] = (weighted_bar * scaled + dot(bucket_bar, hot, precision=PRECISE)).astype(BF16)
+    bar = (weighted_bar * scaled + dot(bucket_bar, hot, precision=PRECISE)).astype(BF16)
     grad = weighted_bar[scen:, :half] * netted[scen:, :half] * conc_factor[scen:, :half]
-    weight_out[...] = jnp.broadcast_to(jnp.sum(grad, axis=0, keepdims=True), weight_out.shape)
-
-
-def pull_kernel(bar, mine, other, where, money, side, state_out):
-    scen, trades = money.shape
-    double = 2 * trades
-    half = side.shape[1]
+    weight = jnp.broadcast_to(jnp.sum(grad, axis=0, keepdims=True), (8, half)).astype(BF16)
+    trades = side_of.shape[0]
     place = where[:1]
     spread = dot_t(bar[:, :half], mine[:double]) + dot_t(bar[:, half:], other[:double])
     pulled = jnp.zeros((scen, double), F32)
@@ -160,7 +155,10 @@
         pulled = pulled + jnp.where(place == w, spread[w * scen : (w + 1) * scen], 0.0)
     likely = lax.logistic(money[...])
     money_bar = (pulled[:, :trades] * likely * (1.0 - likely) + pulled[:, trades:]).astype(BF16)
-    state_out[...] = dot(money_bar, side[...]).astype(BF16)
+    state = dot(money_bar, side_of[...]).astype(BF16)
+    for i in range(out.shape[0]):
+        out[i, :scen] = state
+        out[i, scen:] = weight
 
 
 def near_vmem(x):
@@ -185,13 +183,12 @@
     return lax.ppermute(x, axis, pairs)
 
 
-def sum_over_trades(part):
+def sum_over_trades(copies):
     devs = lax.axis_size("trades")
     blocks = devs // NEAR
     place = lambda b, j: (b * NEAR + j - NEAR // 2) % devs
     mine = ((lax.axis_index("trades") + NEAR // 2) % devs) // NEAR
     groups = [[place(b, j) for j in range(NEAR)] for b in range(blocks)]
-    copies = jnp.broadcast_to(part[None], (NEAR, *part.shape))
     got = lax.all_to_all(copies, "trades", 0, 0, tiled=True, axis_index_groups=groups)
     total = jnp.sum(got.astype(F32), axis=0)
 
@@ -207,9 +204,13 @@
     total = add(total, (3, 1))
     out = total.astype(BF16)
     whole = (total + send(out, (7, 0)).astype(F32) + send(out, (1, 0)).astype(F32)).astype(BF16)
-    first = send(whole, (0, 1))
-    second = send(whole, (0, 2))
-    third = send(whole, (0, 3))
+    def spread(x, target):
+        pairs = [(place(0, NEAR - 1 - j), place(target, j)) for j in range(NEAR)]
+        return lax.ppermute(x, "trades", pairs)
+
+    first = spread(whole, 1)
+    second = spread(whole, 2)
+    third = spread(whole, 3)
     first, second, third = lax.optimization_barrier((first, second, third))
     fourth = send(jnp.where(mine == 3, third, second), (3, 4), (2, 7))
     fifth = send(fourth, (4, 5), (7, 6))
@@ -266,25 +267,23 @@
         ),
         pair, where, mine, other,
     )
-    below = near_vmem(shifted(low, "trades", -1))
-    above = near_vmem(shifted(high, "trades", 1))
+    below, above = lax.optimization_barrier(
+        (shifted(low, "trades", -1), shifted(high, "trades", 1))
+    )
+    below, above = near_vmem(below), near_vmem(above)
     low, mid, high = near_vmem(low), near_vmem(mid), near_vmem(high)
-    bar, weight = call(
+    copies = call(
         sets_kernel,
-        (pltpu.VMEM((SPAN * scen, factors), BF16), pltpu.VMEM((8, half), F32)),
-        low, mid, high, above, below, mine, other, corr, fund, limit,
-    )
-    for step in (1, 2):
-        pairs = [(i, i ^ step) for i in range(lax.axis_size("scen"))]
-        weight = weight + lax.ppermute(weight, "scen", pairs)
-    state_part = call(
-        pull_kernel,
-        pltpu.VMEM((scen, half), BF16),
-        near_vmem(bar), mine, other, where, money, side,
-    )
-    total = sum_over_trades(jnp.concatenate([state_part, weight.astype(BF16)], axis=0)).astype(F32)
-    weight_grad = total[scen] / (scen * lax.axis_size("scen") * set_count)
-    return (total[:scen], weight_grad)
+        pltpu.VMEM((NEAR, scen + 8, half), BF16),
+        low, mid, high, above, below, mine, other, corr, fund, limit, where, money, side,
+    )
+    total = sum_over_trades(copies)
+    cols = lax.axis_size("scen")
+    copies = jnp.broadcast_to(total[scen:][None], (cols, 8, half))
+    weight_sum = jnp.sum(lax.all_to_all(copies, "scen", 0, 0, tiled=True).astype(F32), axis=0)[0]
+    total, weight_sum = lax.optimization_barrier((total, weight_sum))
+    weight_grad = weight_sum / (scen * cols * set_count)
+    return (total[:scen].astype(F32), weight_grad)
 
 
 def solution(mesh):

time: 114 us -> 110 us (0.965)
  blocking collectives: 47.1 us -> 58.7 us
  starting transfers between devices: 26.9 us -> 18.9 us
  waiting for transfers between devices: 32.3 us -> 24.7 us
    all_to_all x0 -> x1, blocking collectives: none -> 9.69 us  [on_device(): lax.all_to_all(copies, 'scen', 0, 0, tiled=True).astype(F32)]
    ppermute x2 -> x3, starting transfers between devices: 8.78 us -> 4.39 us  [spread(): return lax.ppermute(x, 'trades', pairs)]
    ppermute x10 -> x7, starting transfers between devices: 10.2 us -> 5.91 us  [send(): return lax.ppermute(x, 'trades', pairs)]
    ppermute x2, waiting for transfers between devices: 5.29 us -> 1.57 us  [shifted(): return lax.ppermute(x, axis, pairs)]
    ppermute x2 -> x3, waiting for transfers between devices: 3.29 us -> 1.32 us  [spread(): return lax.ppermute(x, 'trades', pairs)]
    all_to_all x1, blocking collectives: 47.1 us -> 49 us  [sum_over_trades(): lax.all_to_all(copies, 'trades', 0, 0, tiled=True, axis_index_groups=groups)]
    ppermute x10 -> x7, waiting for transfers between devices: 23 us -> 21.1 us  [send(): return lax.ppermute(x, 'trades', pairs)]
    pallas_call x5 -> x4, Pallas kernels: 4.97 us -> 5 us  [call(): pl.pallas_call(body, out_shape=out_shape, in_specs=[pl.BlockSpec(memory_s...]
  transfers between devices with their start and end apart: 15 -> 13, of which waited for: 7 -> 4; matrix products, arithmetic and copies ran while one was open for 0% -> 0% of each run, Pallas kernels for 1% -> 1%
where the time goes in v3:
time: 110 us
  blocking collectives  58.7 us (53%)
  waiting for transfers between devices  24.7 us (22%)
  starting transfers between devices  18.9 us (17%)
  Pallas kernels  5 us (5%)
  other arithmetic  1.21 us (1%)
    all_to_all x1, blocking collectives, sum_over_trades(): lax.all_to_all(copies, 'trades', 0, 0, tiled=True, axis_index_groups=groups)  49 us
    ppermute x7, waiting for transfers between devices, send(): return lax.ppermute(x, 'trades', pairs)  21.1 us
    all_to_all x1, blocking collectives, on_device(): lax.all_to_all(copies, 'scen', 0, 0, tiled=True).astype(F32)  9.69 us
    ppermute x2, starting transfers between devices, shifted(): return lax.ppermute(x, axis, pairs)  6.66 us
    ppermute x7, starting transfers between devices, send(): return lax.ppermute(x, 'trades', pairs)  5.91 us
    pallas_call x4, Pallas kernels, call(): pl.pallas_call(body, out_shape=out_shape, in_specs=[pl.BlockSpec(memory_s...  5 us
    ppermute x3, starting transfers between devices, spread(): return lax.ppermute(x, 'trades', pairs)  4.39 us
  transfers between devices with their start and end apart: 13, of which 4 were waited for; matrix products, arithmetic and copies ran while one was open for 0% of the time, Pallas kernels for 1%

profile of v3, /device:TPU:40, one launch (start us, length us, event | category | flops | bytes accessed | tf_op | source)
XLA Modules:
  0.0 109.6 jit_solution(10400743310701504169)
XLA Ops:
  0.7 1.1 %shard_map.114.mine = bf16[1440,128]{1,0:T(8,128)(2,1)S(1)} custom-call(bf16[512,128]{1,0:T(8,128)(2,1)} %load.1, bf16[512,128]{1,0:T(8,128)(2,1)} %curve.1, f32[256,128]{1,0:T(8,128)} %corr.3, f32[1,128]{1,0:T(1,128)} %bitcast.6, s32[1,128]{1,0:T(1,128)} %bitcast.7), custom_call_target="tpu_custom_call" | custom-call | tf_op jit(solution)/shard_map/pallas_call | solution.py:169
  1.8 2.0 %collective-permute-start = (bf16[1440,128]{1,0:T(8,128)(2,1)S(1)}, bf16[1440,128]{1,0:T(8,128)(2,1)S(1)}, u32[]{:S(2)}, u32[]{:S(2)}) collective-permute-start(bf16[1440,128]{1,0:T(8,128)(2,1)S(1)} %shard_map.114.mine), channel_id=1, source_target_pairs={{0,1},{1,0},{2,3},{3,2},{4,5},{5,4},{6,7},{7,6},{8,9},{9,8},{10,11... | collective-permute-start | bytes 1105928 | tf_op jit(solution)/shard_map/ppermute | solution.py:241
  3.8 0.9 shard_map.113
  4.7 0.7 collective-permute-done.other
  5.9 1.3 %collective-permute-start.1 = (f32[32,256]{1,0:T(8,128)S(1)}, f32[32,256]{1,0:T(8,128)S(1)}, u32[]{:S(2)}, u32[]{:S(2)}) collective-permute-start(f32[32,256]{1,0:T(8,128)S(1)} %get-tuple-element.21.low), channel_id=1, source_target_pairs={{8,0},{16,8},{24,16},{32,24},{40,32},{48,40},{56,48},{64,56},{72,6... | collective-permute-start | bytes 98312 | tf_op jit(solution)/shard_map/ppermute | solution.py:183
  7.2 5.4 %collective-permute-start.2 = (f32[32,256]{1,0:T(8,128)S(1)}, f32[32,256]{1,0:T(8,128)S(1)}, u32[]{:S(2)}, u32[]{:S(2)}) collective-permute-start(f32[32,256]{1,0:T(8,128)S(1)} %get-tuple-element.23.high), channel_id=1, source_target_pairs={{0,8},{8,16},{16,24},{24,32},{32,40},{40,48},{48,56},{56,64},{64,7... | collective-permute-start | bytes 98312 | tf_op jit(solution)/shard_map/ppermute | solution.py:183
  12.6 1.6 %collective-permute-done.2.above = f32[32,256]{1,0:T(8,128)S(1)} collective-permute-done((f32[32,256]{1,0:T(8,128)S(1)}, f32[32,256]{1,0:T(8,128)S(1)}, u32[]{:S(2)}, u32[]{:S(2)}) %collective-permute-start.2) | collective-permute-done | bytes 32800 | tf_op jit(solution)/shard_map/ppermute | solution.py:183
  14.2 2.5 %shard_map.116 = bf16[4,40,128]{2,1,0:T(8,128)(2,1)S(1)} custom-call(f32[32,256]{1,0:T(8,128)S(1)} %get-tuple-element.21.low, f32[96,256]{1,0:T(8,128)S(1)} %get-tuple-element.22.mid, f32[32,256]{1,0:T(8,128)S(1)} %get-tuple-element.23.high, f32[32,256]{1,0:T(8,128)S(1)} %collective-permute-done.2.above, f32[32,256]{1,0:T(8,128)S(1)} %collective-permute-done.1.below, ...), custom_call_target="tpu_custom_call" | custom-call | tf_op jit(solution)/shard_map/pallas_call | solution.py:169
  16.7 49.0 %all_to_all.10 = bf16[4,40,128]{2,1,0:T(8,128)(2,1)S(1)} all-to-all(bf16[4,40,128]{2,1,0:T(8,128)(2,1)S(1)} %shard_map.116), channel_id=1, replica_groups={{240,248,0,8},{16,24,32,40},{48,56,64,72},{80,88,96,104},{112,120,128,1..., dimensions={0} | all-to-all | bytes 81920 | tf_op jit(solution)/shard_map/all_to_all | solution.py:192
  65.8 0.7 collective-permute-start.3
  66.5 0.7 collective-permute-start.4
  67.1 0.7 collective-permute-start.5
  67.8 1.3 %collective-permute-start.7 = (bf16[40,128]{1,0:T(8,128)(2,1)S(1)}, bf16[40,128]{1,0:T(8,128)(2,1)S(1)}, u32[]{:S(2)}, u32[]{:S(2)}) collective-permute-start(bf16[40,128]{1,0:T(8,128)(2,1)S(1)} %fusion.1), channel_id=1, source_target_pairs={{16,240},{24,248},{32,0},{40,8},{17,241},{25,249},{33,1},{41,9},{1... | collective-permute-start | bytes 30728 | tf_op jit(solution)/shard_map/ppermute | solution.py:197
  69.2 1.3 %collective-permute-start.6 = (bf16[40,128]{1,0:T(8,128)(2,1)S(1)}, bf16[40,128]{1,0:T(8,128)(2,1)S(1)}, u32[]{:S(2)}, u32[]{:S(2)}) collective-permute-start(bf16[40,128]{1,0:T(8,128)(2,1)S(1)} %fusion.1), channel_id=1, source_target_pairs={{208,240},{216,248},{224,0},{232,8},{209,241},{217,249},{225,1},{2... | collective-permute-start | bytes 30728 | tf_op jit(solution)/shard_map/ppermute | solution.py:197
  70.5 21.1 %collective-permute-done.7 = bf16[40,128]{1,0:T(8,128)(2,1)S(1)} collective-permute-done((bf16[40,128]{1,0:T(8,128)(2,1)S(1)}, bf16[40,128]{1,0:T(8,128)(2,1)S(1)}, u32[]{:S(2)}, u32[]{:S(2)}) %collective-permute-start.7) | collective-permute-done | bytes 10272 | tf_op jit(solution)/shard_map/ppermute | solution.py:197
  91.6 1.8 %collective-permute-start.8 = (bf16[40,128]{1,0:T(8,128)(2,1)S(1)}, bf16[40,128]{1,0:T(8,128)(2,1)S(1)}, u32[]{:S(2)}, u32[]{:S(2)}) collective-permute-start(bf16[40,128]{1,0:T(8,128)(2,1)S(1)} %add_convert_fusion), channel_id=1, source_target_pairs={{8,16},{0,24},{248,32},{240,40},{9,17},{1,25},{249,33},{241,41},{1... | collective-permute-start | bytes 30728 | tf_op jit(solution)/shard_map/ppermute | solution.py:209
  93.4 1.3 %collective-permute-start.9 = (bf16[40,128]{1,0:T(8,128)(2,1)S(1)}, bf16[40,128]{1,0:T(8,128)(2,1)S(1)}, u32[]{:S(2)}, u32[]{:S(2)}) collective-permute-start(bf16[40,128]{1,0:T(8,128)(2,1)S(1)} %add_convert_fusion), channel_id=1, source_target_pairs={{8,48},{0,56},{248,64},{240,72},{9,49},{1,57},{249,65},{241,73},{1... | collective-permute-start | bytes 30728 | tf_op jit(solution)/shard_map/ppermute | solution.py:209
  94.7 1.3 %collective-permute-start.10 = (bf16[40,128]{1,0:T(8,128)(2,1)S(1)}, bf16[40,128]{1,0:T(8,128)(2,1)S(1)}, u32[]{:S(2)}, u32[]{:S(2)}) collective-permute-start(bf16[40,128]{1,0:T(8,128)(2,1)S(1)} %add_convert_fusion), channel_id=1, source_target_pairs={{8,80},{0,88},{248,96},{240,104},{9,81},{1,89},{249,97},{241,105},... | collective-permute-start | bytes 30728 | tf_op jit(solution)/shard_map/ppermute | solution.py:209
  96.1 1.3 %collective-permute-done.10 = bf16[40,128]{1,0:T(8,128)(2,1)S(1)} collective-permute-done((bf16[40,128]{1,0:T(8,128)(2,1)S(1)}, bf16[40,128]{1,0:T(8,128)(2,1)S(1)}, u32[]{:S(2)}, u32[]{:S(2)}) %collective-permute-start.10) | collective-permute-done | bytes 10272 | tf_op jit(solution)/shard_map/ppermute | solution.py:209
  97.4 0.7 collective-permute-start.11
  98.0 0.7 collective-permute-start.12
  98.8 9.7 %all_to_all.11 = bf16[4,8,128]{2,1,0:T(8,128)(2,1)S(1)} all-to-all(bf16[4,8,128]{2,1,0:T(8,128)(2,1)S(1)} %broadcast_in_dim.2), channel_id=1, replica_groups=mesh['groups'=2,'trades'=32,'scen'=4,'fact'=2] {'scen'}, dimensions={0} | all-to-all | bytes 16384 | tf_op jit(solution)/shard_map/all_to_all | solution.py:283
  108.5 0.6 slice_convert_fusion
  109.1 0.5 broadcast_multiply_fusion
  (32 shorter events, 0.6 us)
Async XLA Ops:
  0.6 3.1 %copy-start = (f32[256,128]{1,0:T(8,128)S(1)}, f32[256,128]{1,0:T(8,128)}, u32[]{:S(2)}) copy-start(f32[256,128]{1,0:T(8,128)} %corr.3) | copy-start | bytes 393220
  0.6 3.1 %copy-start.1 = (bf16[512,256]{1,0:T(8,128)(2,1)S(1)}, bf16[512,256]{1,0:T(8,128)(2,1)}, u32[]{:S(2)}) copy-start(bf16[512,256]{1,0:T(8,128)(2,1)} %direction.1) | copy-start | bytes 786436
  0.7 3.1 %copy-start.2 = (bf16[32,256]{1,0:T(8,128)(2,1)S(1)}, bf16[32,256]{1,0:T(8,128)(2,1)}, u32[]{:S(2)}) copy-start(bf16[32,256]{1,0:T(8,128)(2,1)} %state.1) | copy-start | bytes 49156
  0.7 3.1 %copy-start.3 = (f32[32,128]{1,0:T(8,128)S(1)}, f32[32,128]{1,0:T(8,128)}, u32[]{:S(2)}) copy-start(f32[32,128]{1,0:T(8,128)} %funding.1) | copy-start | bytes 49156
  0.7 3.1 %copy-start.4 = (s32[512]{0:T(512)S(1)}, s32[512]{0:T(512)}, u32[]{:S(2)}) copy-start(s32[512]{0:T(512)} %param.14) | copy-start | bytes 6148
  1.8 3.6 %collective-permute-start = (bf16[1440,128]{1,0:T(8,128)(2,1)S(1)}, bf16[1440,128]{1,0:T(8,128)(2,1)S(1)}, u32[]{:S(2)}, u32[]{:S(2)}) collective-permute-start(bf16[1440,128]{1,0:T(8,128)(2,1)S(1)} %shard_map.114.mine), channel_id=1, source_target_pairs={{0,1},{1,0},{2,3},{3,2},{4,5},{5,4},{6,7},{7,6},{8,9},{9,8},{10,11... | collective-permute-start | bytes 1105928 | tf_op jit(solution)/shard_map/ppermute | solution.py:241
  5.9 6.7 %collective-permute-start.1 = (f32[32,256]{1,0:T(8,128)S(1)}, f32[32,256]{1,0:T(8,128)S(1)}, u32[]{:S(2)}, u32[]{:S(2)}) collective-permute-start(f32[32,256]{1,0:T(8,128)S(1)} %get-tuple-element.21.low), channel_id=1, source_target_pairs={{8,0},{16,8},{24,16},{32,24},{40,32},{48,40},{56,48},{64,56},{72,6... | collective-permute-start | bytes 98312 | tf_op jit(solution)/shard_map/ppermute | solution.py:183
  7.2 6.9 %collective-permute-start.2 = (f32[32,256]{1,0:T(8,128)S(1)}, f32[32,256]{1,0:T(8,128)S(1)}, u32[]{:S(2)}, u32[]{:S(2)}) collective-permute-start(f32[32,256]{1,0:T(8,128)S(1)} %get-tuple-element.23.high), channel_id=1, source_target_pairs={{0,8},{8,16},{16,24},{24,32},{32,40},{40,48},{48,56},{56,64},{64,7... | collective-permute-start | bytes 98312 | tf_op jit(solution)/shard_map/ppermute | solution.py:183
  65.8 0.7 collective-permute-start.3
  66.5 0.7 collective-permute-start.4
  67.1 0.7 collective-permute-start.5
  67.8 23.7 %collective-permute-start.7 = (bf16[40,128]{1,0:T(8,128)(2,1)S(1)}, bf16[40,128]{1,0:T(8,128)(2,1)S(1)}, u32[]{:S(2)}, u32[]{:S(2)}) collective-permute-start(bf16[40,128]{1,0:T(8,128)(2,1)S(1)} %fusion.1), channel_id=1, source_target_pairs={{16,240},{24,248},{32,0},{40,8},{17,241},{25,249},{33,1},{41,9},{1... | collective-permute-start | bytes 30728 | tf_op jit(solution)/shard_map/ppermute | solution.py:197
  69.2 22.4 %collective-permute-start.6 = (bf16[40,128]{1,0:T(8,128)(2,1)S(1)}, bf16[40,128]{1,0:T(8,128)(2,1)S(1)}, u32[]{:S(2)}, u32[]{:S(2)}) collective-permute-start(bf16[40,128]{1,0:T(8,128)(2,1)S(1)} %fusion.1), channel_id=1, source_target_pairs={{208,240},{216,248},{224,0},{232,8},{209,241},{217,249},{225,1},{2... | collective-permute-start | bytes 30728 | tf_op jit(solution)/shard_map/ppermute | solution.py:197
  91.6 4.5 %collective-permute-start.8 = (bf16[40,128]{1,0:T(8,128)(2,1)S(1)}, bf16[40,128]{1,0:T(8,128)(2,1)S(1)}, u32[]{:S(2)}, u32[]{:S(2)}) collective-permute-start(bf16[40,128]{1,0:T(8,128)(2,1)S(1)} %add_convert_fusion), channel_id=1, source_target_pairs={{8,16},{0,24},{248,32},{240,40},{9,17},{1,25},{249,33},{241,41},{1... | collective-permute-start | bytes 30728 | tf_op jit(solution)/shard_map/ppermute | solution.py:209
  93.4 2.7 %collective-permute-start.9 = (bf16[40,128]{1,0:T(8,128)(2,1)S(1)}, bf16[40,128]{1,0:T(8,128)(2,1)S(1)}, u32[]{:S(2)}, u32[]{:S(2)}) collective-permute-start(bf16[40,128]{1,0:T(8,128)(2,1)S(1)} %add_convert_fusion), channel_id=1, source_target_pairs={{8,48},{0,56},{248,64},{240,72},{9,49},{1,57},{249,65},{241,73},{1... | collective-permute-start | bytes 30728 | tf_op jit(solution)/shard_map/ppermute | solution.py:209
  94.7 2.7 %collective-permute-start.10 = (bf16[40,128]{1,0:T(8,128)(2,1)S(1)}, bf16[40,128]{1,0:T(8,128)(2,1)S(1)}, u32[]{:S(2)}, u32[]{:S(2)}) collective-permute-start(bf16[40,128]{1,0:T(8,128)(2,1)S(1)} %add_convert_fusion), channel_id=1, source_target_pairs={{8,80},{0,88},{248,96},{240,104},{9,81},{1,89},{249,97},{241,105},... | collective-permute-start | bytes 30728 | tf_op jit(solution)/shard_map/ppermute | solution.py:209
  97.4 0.7 collective-permute-start.11
  98.0 0.7 collective-permute-start.12

commit v4 on v3

--- a/solution.py
+++ b/solution.py
@@ -1,3 +1,5 @@
+import functools
+
 import jax
 import jax.numpy as jnp
 from jax import lax
@@ -161,6 +163,31 @@
         out[i, scen:] = weight
 
 
+def fold_kernel(got, total_out):
+    count, rows, half = got.shape
+    cols = count // NEAR
+    scen = rows - 8
+    mine = lax.axis_index("scen")
+    state = jnp.zeros((scen, half), F32)
+    for j in range(NEAR):
+        state = state + got[j * cols + mine, :scen].astype(F32)
+    weight = jnp.zeros((8, half), F32)
+    for i in range(count):
+        weight = weight + got[i, scen:].astype(F32)
+    total_out[:scen] = state
+    total_out[scen:] = weight
+
+
+def last_kernel(count, whole, first, second, third, fourth, state_out, weight_out):
+    scen = state_out.shape[0]
+    devs = lax.axis_size("trades")
+    late = lax.rem(lax.axis_index("trades") + NEAR // 2, devs) < NEAR
+    parts = [x[...].astype(F32) for x in (whole, first, second, third, fourth)]
+    total = jnp.where(late, parts[0], parts[1] + parts[2] + parts[3] + parts[4])
+    state_out[...] = total[:scen]
+    weight_out[...] = total[scen : scen + 1] * (1.0 / count)
+
+
 def near_vmem(x):
     return pltpu.with_memory_space_constraint(x, pltpu.VMEM)
 
@@ -184,37 +211,34 @@
 
 
 def sum_over_trades(copies):
-    devs = lax.axis_size("trades")
+    devs, cols = lax.axis_size("trades"), lax.axis_size("scen")
     blocks = devs // NEAR
     place = lambda b, j: (b * NEAR + j - NEAR // 2) % devs
-    mine = ((lax.axis_index("trades") + NEAR // 2) % devs) // NEAR
-    groups = [[place(b, j) for j in range(NEAR)] for b in range(blocks)]
-    got = lax.all_to_all(copies, "trades", 0, 0, tiled=True, axis_index_groups=groups)
-    total = jnp.sum(got.astype(F32), axis=0)
+    mine = lax.rem(lax.axis_index("trades") + NEAR // 2, devs) // NEAR
+    groups = [
+        [place(b, j) * cols + c for j in range(NEAR) for c in range(cols)] for b in range(blocks)
+    ]
+    got = lax.all_to_all(copies, ("trades", "scen"), 0, 0, tiled=True, axis_index_groups=groups)
+    total = call(fold_kernel, pltpu.VMEM(copies.shape[1:], F32), near_vmem(got))
 
     def send(x, *links):
-        pairs = [(place(a, j), place(b, j)) for a, b in links for j in range(NEAR)]
-        return lax.ppermute(x, "trades", pairs)
-
-    def add(x, *links):
-        return x + send(x.astype(BF16), *links).astype(F32)
-
-    total = add(total, (4, 3), (2, 1))
-    total = add(total, (5, 3), (6, 7))
-    total = add(total, (3, 1))
-    out = total.astype(BF16)
-    whole = (total + send(out, (7, 0)).astype(F32) + send(out, (1, 0)).astype(F32)).astype(BF16)
-    def spread(x, target):
-        pairs = [(place(0, NEAR - 1 - j), place(target, j)) for j in range(NEAR)]
-        return lax.ppermute(x, "trades", pairs)
-
-    first = spread(whole, 1)
-    second = spread(whole, 2)
-    third = spread(whole, 3)
-    first, second, third = lax.optimization_barrier((first, second, third))
-    fourth = send(jnp.where(mine == 3, third, second), (3, 4), (2, 7))
-    fifth = send(fourth, (4, 5), (7, 6))
-    return jnp.where(mine == 0, whole, first + second + third + fourth + fifth)
+        pairs = []
+        for a, b, flip in links:
+            pairs += [(place(a, NEAR - 1 - j if flip else j), place(b, j)) for j in range(NEAR)]
+        return lax.ppermute(x.astype(BF16), "trades", pairs)
+
+    total = total + send(total, (4, 3, 0), (2, 1, 0)).astype(F32)
+    one, two = lax.optimization_barrier(
+        (send(total, (5, 1, 0), (6, 7, 0)), send(total, (3, 1, 0)))
+    )
+    total = total + one.astype(F32) + two.astype(F32)
+    one, two = lax.optimization_barrier((send(total, (7, 0, 0)), send(total, (1, 0, 0))))
+    whole = (total + one.astype(F32) + two.astype(F32)).astype(BF16)
+    first, second = lax.optimization_barrier((send(whole, (0, 1, 1)), send(whole, (0, 2, 1))))
+    have = jnp.where(mine == 1, first, jnp.where(mine == 2, second, whole))
+    third = send(have, (0, 4, 1), (1, 3, 0), (2, 7, 0))
+    fourth = send(third, (4, 5, 0), (7, 6, 0))
+    return whole, first, second, third, fourth
 
 
 def on_device(
@@ -274,16 +298,16 @@
     low, mid, high = near_vmem(low), near_vmem(mid), near_vmem(high)
     copies = call(
         sets_kernel,
-        pltpu.VMEM((NEAR, scen + 8, half), BF16),
+        pltpu.VMEM((NEAR * lax.axis_size("scen"), scen + 8, half), BF16),
         low, mid, high, above, below, mine, other, corr, fund, limit, where, money, side,
     )
-    total = sum_over_trades(copies)
-    cols = lax.axis_size("scen")
-    copies = jnp.broadcast_to(total[scen:][None], (cols, 8, half))
-    weight_sum = jnp.sum(lax.all_to_all(copies, "scen", 0, 0, tiled=True).astype(F32), axis=0)[0]
-    total, weight_sum = lax.optimization_barrier((total, weight_sum))
-    weight_grad = weight_sum / (scen * cols * set_count)
-    return (total[:scen].astype(F32), weight_grad)
+    count = scen * lax.axis_size("scen") * set_count
+    state_grad, weight_grad = call(
+        functools.partial(last_kernel, count),
+        (jax.ShapeDtypeStruct((scen, half), F32), jax.ShapeDtypeStruct((1, half), F32)),
+        *map(near_vmem, sum_over_trades(copies)),
+    )
+    return (state_grad, weight_grad.reshape(half))
 
 
 def solution(mesh):

time: 110 us -> 115 us (1.045)
  the two profiles are of different devices: /device:TPU:40 before, /device:TPU:34 now
where the time goes in v4:
time: 115 us; the launch traced here: 114 us
  blocking collectives  53.8 us (47%)
  waiting for transfers between devices  36.1 us (31%)
  starting transfers between devices  17.8 us (15%)
  Pallas kernels  5.65 us (5%)
    all_to_all x1, blocking collectives, sum_over_trades(): lax.all_to_all(copies, ('trades', 'scen'), 0, 0, tiled=True, axis_index_g...  53.8 us
    ppermute x9, waiting for transfers between devices, send(): return lax.ppermute(x.astype(BF16), 'trades', pairs)  33.8 us
    ppermute x9, starting transfers between devices, send(): return lax.ppermute(x.astype(BF16), 'trades', pairs)  9.17 us
    ppermute x2, starting transfers between devices, shifted(): return lax.ppermute(x, axis, pairs)  6.66 us
    pallas_call x6, Pallas kernels, call(): pl.pallas_call(body, out_shape=out_shape, in_specs=[pl.BlockSpec(memory_s...  5.65 us
  transfers between devices with their start and end apart: 12, of which 6 were waited for; matrix products, arithmetic and copies ran while one was open for 0% of the time, Pallas kernels for 1%

profile of v4, /device:TPU:34, one launch (start us, length us, event | category | flops | bytes accessed | tf_op | source)
XLA Modules:
  0.0 114.3 jit_solution(4827802230403645025)
XLA Ops:
  0.7 1.1 shard_map.114.mine
  1.8 2.0 %collective-permute-start = (bf16[1440,128]{1,0:T(8,128)(2,1)S(1)}, bf16[1440,128]{1,0:T(8,128)(2,1)S(1)}, u32[]{:S(2)}, u32[]{:S(2)}) collective-permute-start(bf16[1440,128]{1,0:T(8,128)(2,1)S(1)} %shard_map.114.mine), channel_id=1, source_target_pairs={{0,1},{1,0},{2,3},{3,2},{4,5},{5,4},{6,7},{7,6},{8,9},{9,8},{10,11... | collective-permute-start | bytes 1105928 | tf_op jit(solution)/shard_map/ppermute | solution.py:265
  3.8 0.9 shard_map.113
  4.7 0.7 collective-permute-done.other
  5.4 0.5 shard_map.115
  5.9 1.3 %collective-permute-start.1 = (f32[32,256]{1,0:T(8,128)S(1)}, f32[32,256]{1,0:T(8,128)S(1)}, u32[]{:S(2)}, u32[]{:S(2)}) collective-permute-start(f32[32,256]{1,0:T(8,128)S(1)} %get-tuple-element.24.low), channel_id=1, source_target_pairs={{8,0},{16,8},{24,16},{32,24},{40,32},{48,40},{56,48},{64,56},{72,6... | collective-permute-start | bytes 98312 | tf_op jit(solution)/shard_map/ppermute | solution.py:210
  7.2 5.4 %collective-permute-start.2 = (f32[32,256]{1,0:T(8,128)S(1)}, f32[32,256]{1,0:T(8,128)S(1)}, u32[]{:S(2)}, u32[]{:S(2)}) collective-permute-start(f32[32,256]{1,0:T(8,128)S(1)} %get-tuple-element.26.high), channel_id=1, source_target_pairs={{0,8},{8,16},{16,24},{24,32},{32,40},{40,48},{48,56},{56,64},{64,7... | collective-permute-start | bytes 98312 | tf_op jit(solution)/shard_map/ppermute | solution.py:210
  12.6 1.6 %collective-permute-done.2.above = f32[32,256]{1,0:T(8,128)S(1)} collective-permute-done((f32[32,256]{1,0:T(8,128)S(1)}, f32[32,256]{1,0:T(8,128)S(1)}, u32[]{:S(2)}, u32[]{:S(2)}) %collective-permute-start.2) | collective-permute-done | bytes 32800 | tf_op jit(solution)/shard_map/ppermute | solution.py:210
  14.2 2.5 %shard_map.116 = bf16[16,40,128]{2,1,0:T(8,128)(2,1)S(1)} custom-call(f32[32,256]{1,0:T(8,128)S(1)} %get-tuple-element.24.low, f32[96,256]{1,0:T(8,128)S(1)} %get-tuple-element.25.mid, f32[32,256]{1,0:T(8,128)S(1)} %get-tuple-element.26.high, f32[32,256]{1,0:T(8,128)S(1)} %collective-permute-done.2.above, f32[32,256]{1,0:T(8,128)S(1)} %collective-permute-done.1.below, ...), custom_call_target="tpu_custom_call" | custom-call | tf_op jit(solution)/shard_map/pallas_call | solution.py:196
  16.7 53.8 %all_to_all.5.got = bf16[16,40,128]{2,1,0:T(8,128)(2,1)S(1)} all-to-all(bf16[16,40,128]{2,1,0:T(8,128)(2,1)S(1)} %shard_map.116), channel_id=1, replica_groups={{240,242,244,246,248,250,252,254,0,2,4,6,8,10,12,14},{16,18,20,22,24,26..., dimensions={0} | all-to-all | bytes 327680 | tf_op jit(solution)/shard_map/all_to_all | solution.py:221
  70.5 0.7 collective-permute-start.3
  71.2 0.7 collective-permute-start.4
  71.9 0.7 collective-permute-start.5
  72.6 1.3 %collective-permute-start.6 = (bf16[40,128]{1,0:T(8,128)(2,1)S(1)}, bf16[40,128]{1,0:T(8,128)(2,1)S(1)}, u32[]{:S(2)}, u32[]{:S(2)}) collective-permute-start(bf16[40,128]{1,0:T(8,128)(2,1)S(1)} %fusion.1), channel_id=1, source_target_pairs={{208,240},{216,248},{224,0},{232,8},{209,241},{217,249},{225,1},{2... | collective-permute-start | bytes 30728 | tf_op jit(solution)/shard_map/ppermute | solution.py:228
  73.9 1.3 %collective-permute-start.7 = (bf16[40,128]{1,0:T(8,128)(2,1)S(1)}, bf16[40,128]{1,0:T(8,128)(2,1)S(1)}, u32[]{:S(2)}, u32[]{:S(2)}) collective-permute-start(bf16[40,128]{1,0:T(8,128)(2,1)S(1)} %fusion.1), channel_id=1, source_target_pairs={{16,240},{24,248},{32,0},{40,8},{17,241},{25,249},{33,1},{41,9},{1... | collective-permute-start | bytes 30728 | tf_op jit(solution)/shard_map/ppermute | solution.py:228
  75.2 12.3 %collective-permute-done.6 = bf16[40,128]{1,0:T(8,128)(2,1)S(1)} collective-permute-done((bf16[40,128]{1,0:T(8,128)(2,1)S(1)}, bf16[40,128]{1,0:T(8,128)(2,1)S(1)}, u32[]{:S(2)}, u32[]{:S(2)}) %collective-permute-start.6) | collective-permute-done | bytes 10272 | tf_op jit(solution)/shard_map/ppermute | solution.py:228
  87.5 18.8 %collective-permute-done.7 = bf16[40,128]{1,0:T(8,128)(2,1)S(1)} collective-permute-done((bf16[40,128]{1,0:T(8,128)(2,1)S(1)}, bf16[40,128]{1,0:T(8,128)(2,1)S(1)}, u32[]{:S(2)}, u32[]{:S(2)}) %collective-permute-start.7) | collective-permute-done | bytes 10272 | tf_op jit(solution)/shard_map/ppermute | solution.py:228
  106.3 1.3 %collective-permute-start.8 = (bf16[40,128]{1,0:T(8,128)(2,1)S(1)}, bf16[40,128]{1,0:T(8,128)(2,1)S(1)}, u32[]{:S(2)}, u32[]{:S(2)}) collective-permute-start(bf16[40,128]{1,0:T(8,128)(2,1)S(1)} %add_convert_fusion.whole), channel_id=1, source_target_pairs={{8,16},{0,24},{248,32},{240,40},{9,17},{1,25},{249,33},{241,41},{1... | collective-permute-start | bytes 30728 | tf_op jit(solution)/shard_map/ppermute | solution.py:228
  107.6 1.3 %collective-permute-start.9 = (bf16[40,128]{1,0:T(8,128)(2,1)S(1)}, bf16[40,128]{1,0:T(8,128)(2,1)S(1)}, u32[]{:S(2)}, u32[]{:S(2)}) collective-permute-start(bf16[40,128]{1,0:T(8,128)(2,1)S(1)} %add_convert_fusion.whole), channel_id=1, source_target_pairs={{8,48},{0,56},{248,64},{240,72},{9,49},{1,57},{249,65},{241,73},{1... | collective-permute-start | bytes 30728 | tf_op jit(solution)/shard_map/ppermute | solution.py:228
  109.0 1.3 %collective-permute-done.9.second = bf16[40,128]{1,0:T(8,128)(2,1)S(1)} collective-permute-done((bf16[40,128]{1,0:T(8,128)(2,1)S(1)}, bf16[40,128]{1,0:T(8,128)(2,1)S(1)}, u32[]{:S(2)}, u32[]{:S(2)}) %collective-permute-start.9) | collective-permute-done | bytes 10272 | tf_op jit(solution)/shard_map/ppermute | solution.py:228
  110.3 1.3 %collective-permute-start.10 = (bf16[40,128]{1,0:T(8,128)(2,1)S(1)}, bf16[40,128]{1,0:T(8,128)(2,1)S(1)}, u32[]{:S(2)}, u32[]{:S(2)}) collective-permute-start(bf16[40,128]{1,0:T(8,128)(2,1)S(1)} %select_select_fusion), channel_id=1, source_target_pairs={{8,112},{0,120},{248,128},{240,136},{16,80},{24,88},{32,96},{40,10... | collective-permute-start | bytes 30728 | tf_op jit(solution)/shard_map/ppermute | solution.py:228
  111.6 1.4 %collective-permute-done.10.third = bf16[40,128]{1,0:T(8,128)(2,1)S(1)} collective-permute-done((bf16[40,128]{1,0:T(8,128)(2,1)S(1)}, bf16[40,128]{1,0:T(8,128)(2,1)S(1)}, u32[]{:S(2)}, u32[]{:S(2)}) %collective-permute-start.10) | collective-permute-done | bytes 10272 | tf_op jit(solution)/shard_map/ppermute | solution.py:228
  113.0 0.7 collective-permute-start.11
  113.7 0.6 shard_map.118
  (22 shorter events, 0.1 us)
Async XLA Ops:
  0.6 3.1 %copy-start = (f32[256,128]{1,0:T(8,128)S(1)}, f32[256,128]{1,0:T(8,128)}, u32[]{:S(2)}) copy-start(f32[256,128]{1,0:T(8,128)} %corr.3) | copy-start | bytes 393220
  0.6 3.1 %copy-start.1 = (bf16[512,256]{1,0:T(8,128)(2,1)S(1)}, bf16[512,256]{1,0:T(8,128)(2,1)}, u32[]{:S(2)}) copy-start(bf16[512,256]{1,0:T(8,128)(2,1)} %direction.1) | copy-start | bytes 786436
  0.7 3.1 %copy-start.2 = (bf16[32,256]{1,0:T(8,128)(2,1)S(1)}, bf16[32,256]{1,0:T(8,128)(2,1)}, u32[]{:S(2)}) copy-start(bf16[32,256]{1,0:T(8,128)(2,1)} %state.1) | copy-start | bytes 49156
  0.7 3.1 %copy-start.3 = (f32[32,128]{1,0:T(8,128)S(1)}, f32[32,128]{1,0:T(8,128)}, u32[]{:S(2)}) copy-start(f32[32,128]{1,0:T(8,128)} %funding.1) | copy-start | bytes 49156
  0.7 3.1 %copy-start.4 = (s32[512]{0:T(512)S(1)}, s32[512]{0:T(512)}, u32[]{:S(2)}) copy-start(s32[512]{0:T(512)} %param.14) | copy-start | bytes 6148
  1.8 3.6 %collective-permute-start = (bf16[1440,128]{1,0:T(8,128)(2,1)S(1)}, bf16[1440,128]{1,0:T(8,128)(2,1)S(1)}, u32[]{:S(2)}, u32[]{:S(2)}) collective-permute-start(bf16[1440,128]{1,0:T(8,128)(2,1)S(1)} %shard_map.114.mine), channel_id=1, source_target_pairs={{0,1},{1,0},{2,3},{3,2},{4,5},{5,4},{6,7},{7,6},{8,9},{9,8},{10,11... | collective-permute-start | bytes 1105928 | tf_op jit(solution)/shard_map/ppermute | solution.py:265
  5.9 6.7 %collective-permute-start.1 = (f32[32,256]{1,0:T(8,128)S(1)}, f32[32,256]{1,0:T(8,128)S(1)}, u32[]{:S(2)}, u32[]{:S(2)}) collective-permute-start(f32[32,256]{1,0:T(8,128)S(1)} %get-tuple-element.24.low), channel_id=1, source_target_pairs={{8,0},{16,8},{24,16},{32,24},{40,32},{48,40},{56,48},{64,56},{72,6... | collective-permute-start | bytes 98312 | tf_op jit(solution)/shard_map/ppermute | solution.py:210
  7.2 6.9 %collective-permute-start.2 = (f32[32,256]{1,0:T(8,128)S(1)}, f32[32,256]{1,0:T(8,128)S(1)}, u32[]{:S(2)}, u32[]{:S(2)}) collective-permute-start(f32[32,256]{1,0:T(8,128)S(1)} %get-tuple-element.26.high), channel_id=1, source_target_pairs={{0,8},{8,16},{16,24},{24,32},{32,40},{40,48},{48,56},{56,64},{64,7... | collective-permute-start | bytes 98312 | tf_op jit(solution)/shard_map/ppermute | solution.py:210
  70.5 0.7 collective-permute-start.3
  71.2 1.3 %collective-permute-start.4 = (bf16[40,128]{1,0:T(8,128)(2,1)S(1)}, bf16[40,128]{1,0:T(8,128)(2,1)S(1)}, u32[]{:S(2)}, u32[]{:S(2)}) collective-permute-start(bf16[40,128]{1,0:T(8,128)(2,1)S(1)} %fusion), channel_id=1, source_target_pairs={{144,16},{152,24},{160,32},{168,40},{176,208},{184,216},{192,224},... | collective-permute-start | bytes 30728 | tf_op jit(solution)/shard_map/ppermute | solution.py:228
  71.9 0.7 collective-permute-start.5
  72.6 14.9 %collective-permute-start.6 = (bf16[40,128]{1,0:T(8,128)(2,1)S(1)}, bf16[40,128]{1,0:T(8,128)(2,1)S(1)}, u32[]{:S(2)}, u32[]{:S(2)}) collective-permute-start(bf16[40,128]{1,0:T(8,128)(2,1)S(1)} %fusion.1), channel_id=1, source_target_pairs={{208,240},{216,248},{224,0},{232,8},{209,241},{217,249},{225,1},{2... | collective-permute-start | bytes 30728 | tf_op jit(solution)/shard_map/ppermute | solution.py:228
  73.9 32.4 %collective-permute-start.7 = (bf16[40,128]{1,0:T(8,128)(2,1)S(1)}, bf16[40,128]{1,0:T(8,128)(2,1)S(1)}, u32[]{:S(2)}, u32[]{:S(2)}) collective-permute-start(bf16[40,128]{1,0:T(8,128)(2,1)S(1)} %fusion.1), channel_id=1, source_target_pairs={{16,240},{24,248},{32,0},{40,8},{17,241},{25,249},{33,1},{41,9},{1... | collective-permute-start | bytes 30728 | tf_op jit(solution)/shard_map/ppermute | solution.py:228
  106.3 2.7 %collective-permute-start.8 = (bf16[40,128]{1,0:T(8,128)(2,1)S(1)}, bf16[40,128]{1,0:T(8,128)(2,1)S(1)}, u32[]{:S(2)}, u32[]{:S(2)}) collective-permute-start(bf16[40,128]{1,0:T(8,128)(2,1)S(1)} %add_convert_fusion.whole), channel_id=1, source_target_pairs={{8,16},{0,24},{248,32},{240,40},{9,17},{1,25},{249,33},{241,41},{1... | collective-permute-start | bytes 30728 | tf_op jit(solution)/shard_map/ppermute | solution.py:228
  107.6 2.7 %collective-permute-start.9 = (bf16[40,128]{1,0:T(8,128)(2,1)S(1)}, bf16[40,128]{1,0:T(8,128)(2,1)S(1)}, u32[]{:S(2)}, u32[]{:S(2)}) collective-permute-start(bf16[40,128]{1,0:T(8,128)(2,1)S(1)} %add_convert_fusion.whole), channel_id=1, source_target_pairs={{8,48},{0,56},{248,64},{240,72},{9,49},{1,57},{249,65},{241,73},{1... | collective-permute-start | bytes 30728 | tf_op jit(solution)/shard_map/ppermute | solution.py:228
  110.3 2.7 %collective-permute-start.10 = (bf16[40,128]{1,0:T(8,128)(2,1)S(1)}, bf16[40,128]{1,0:T(8,128)(2,1)S(1)}, u32[]{:S(2)}, u32[]{:S(2)}) collective-permute-start(bf16[40,128]{1,0:T(8,128)(2,1)S(1)} %select_select_fusion), channel_id=1, source_target_pairs={{8,112},{0,120},{248,128},{240,136},{16,80},{24,88},{32,96},{40,10... | collective-permute-start | bytes 30728 | tf_op jit(solution)/shard_map/ppermute | solution.py:228
  113.0 0.7 collective-permute-start.11

commit v5 on v4

--- a/solution.py
+++ b/solution.py
@@ -73,7 +73,7 @@
     limit_out[...] = limit
 
 
-def window_kernel(pair, where, mine, other, low_out, mid_out, high_out):
+def window_kernel(pair, where, mine, other, low_out, mid_out, high_out, edge_out):
     scen, double = pair.shape
     paired = pair[...]
     place = where[:1]
@@ -89,17 +89,18 @@
             out, at = high_out, 0
         out[at : at + scen, :half] = dot(mixing, mine[:double])
         out[at : at + scen, half:] = dot(mixing, other[:double])
+    edge_out[...] = low_out[...]
 
 
 def sets_kernel(
-    low, mid, high, above, below, mine, other, corr, fund, limits, where, money, side_of, out
+    low, mid, high, above, below, start, mine, other, corr, fund, limits, where, money, side_of, out
 ):
     scen, factors = low.shape
     half = factors // 2
     double = mine.shape[0] - 3 * half - 32
     side = pl.multiple_of(lax.axis_index("fact") * half, half)
     far_side = pl.multiple_of((1 - lax.axis_index("fact")) * half, half)
-    netted = jnp.concatenate([low[...] + above[...], mid[...], high[...] + below[...]], axis=0)
+    netted = jnp.concatenate([low[...] + above[...], mid[...], high[...] + (below[...] + start[...])], axis=0)
     base = double + 3 * half
 
     def risk_of(ref):
@@ -204,9 +205,9 @@
     )(*args)
 
 
-def shifted(x, axis, by):
+def shifted(x, axis, by, first=0):
     size = lax.axis_size(axis)
-    pairs = [(i, i + by) for i in range(size) if 0 <= i + by < size]
+    pairs = [(i, i + by) for i in range(first, size) if 0 <= i + by < size]
     return lax.ppermute(x, axis, pairs)
 
 
@@ -227,17 +228,14 @@
             pairs += [(place(a, NEAR - 1 - j if flip else j), place(b, j)) for j in range(NEAR)]
         return lax.ppermute(x.astype(BF16), "trades", pairs)
 
-    total = total + send(total, (4, 3, 0), (2, 1, 0)).astype(F32)
-    one, two = lax.optimization_barrier(
-        (send(total, (5, 1, 0), (6, 7, 0)), send(total, (3, 1, 0)))
-    )
-    total = total + one.astype(F32) + two.astype(F32)
+    far = send(total, (5, 1, 0))
+    total = total + send(total, (6, 7, 0), (4, 3, 0), (2, 1, 0)).astype(F32)
+    total = total + far.astype(F32) + send(total, (3, 1, 0)).astype(F32)
     one, two = lax.optimization_barrier((send(total, (7, 0, 0)), send(total, (1, 0, 0))))
     whole = (total + one.astype(F32) + two.astype(F32)).astype(BF16)
-    first, second = lax.optimization_barrier((send(whole, (0, 1, 1)), send(whole, (0, 2, 1))))
-    have = jnp.where(mine == 1, first, jnp.where(mine == 2, second, whole))
-    third = send(have, (0, 4, 1), (1, 3, 0), (2, 7, 0))
-    fourth = send(third, (4, 5, 0), (7, 6, 0))
+    second, first = lax.optimization_barrier((send(whole, (0, 2, 1)), send(whole, (0, 1, 1))))
+    third = send(jnp.where(mine == 1, first, second), (1, 3, 0), (2, 5, 0))
+    fourth = send(jnp.where(mine == 2, second, third), (3, 4, 0), (5, 6, 0), (2, 7, 0))
     return whole, first, second, third, fourth
 
 
@@ -282,24 +280,25 @@
     money, pair, side, corr, where, fund, limit = map(
         near_vmem, (money, pair, side, corr, where, fund, limit)
     )
-    low, mid, high = call(
+    low, mid, high, edge = call(
         window_kernel,
         (
             pltpu.VMEM((scen, factors), F32),
             pltpu.VMEM(((SPAN - 2) * scen, factors), F32),
             pltpu.VMEM((scen, factors), F32),
+            pltpu.VMEM((scen, factors), F32),
         ),
         pair, where, mine, other,
     )
-    below, above = lax.optimization_barrier(
-        (shifted(low, "trades", -1), shifted(high, "trades", 1))
-    )
-    below, above = near_vmem(below), near_vmem(above)
+    below, above, start = lax.optimization_barrier(
+        (shifted(low, "trades", -1, 2), shifted(high, "trades", 1), lax.ppermute(edge, "trades", [(1, 0)]))
+    )
+    below, above, start = near_vmem(below), near_vmem(above), near_vmem(start)
     low, mid, high = near_vmem(low), near_vmem(mid), near_vmem(high)
     copies = call(
         sets_kernel,
         pltpu.VMEM((NEAR * lax.axis_size("scen"), scen + 8, half), BF16),
-        low, mid, high, above, below, mine, other, corr, fund, limit, where, money, side,
+        low, mid, high, above, below, start, mine, other, corr, fund, limit, where, money, side,
     )
     count = scen * lax.axis_size("scen") * set_count
     state_grad, weight_grad = call(

time: 115 us -> 95 us (0.83)
  the two profiles are of different devices: /device:TPU:34 before, /device:TPU:40 now
where the time goes in v5:
time: 95 us; the launch traced here: 94.7 us
  blocking collectives  50.5 us (53%)
  waiting for transfers between devices  19.7 us (21%)
  starting transfers between devices  17.8 us (19%)
  Pallas kernels  5.65 us (6%)
  between operations  0.96 us (1%)
    all_to_all x1, blocking collectives, sum_over_trades(): lax.all_to_all(copies, ('trades', 'scen'), 0, 0, tiled=True, axis_index_g...  50.5 us
    ppermute x9, waiting for transfers between devices, send(): return lax.ppermute(x.astype(BF16), 'trades', pairs)  13.7 us
    ppermute x9, starting transfers between devices, send(): return lax.ppermute(x.astype(BF16), 'trades', pairs)  8.52 us
    ppermute x2, starting transfers between devices, shifted(): return lax.ppermute(x, axis, pairs)  6.02 us
    pallas_call x6, Pallas kernels, call(): pl.pallas_call(body, out_shape=out_shape, in_specs=[pl.BlockSpec(memory_s...  5.65 us
    ppermute x1, waiting for transfers between devices, on_device(): lax.ppermute(edge, 'trades', [(1, 0)])  5.03 us
    ppermute x1, starting transfers between devices, on_device(): other = lax.ppermute(mine, 'fact', [(0, 1), (1, 0)])  1.95 us
  transfers between devices with their start and end apart: 13, of which 5 were waited for; matrix products, arithmetic and copies ran while one was open for 0% of the time, Pallas kernels for 1%

profile of v5, /device:TPU:40, one launch (start us, length us, event | category | flops | bytes accessed | tf_op | source)
XLA Modules:
  0.0 94.7 jit_solution(1152370181609836963)
XLA Ops:
  0.7 1.1 %shard_map.114.mine = bf16[1440,128]{1,0:T(8,128)(2,1)S(1)} custom-call(bf16[512,128]{1,0:T(8,128)(2,1)} %load.1, bf16[512,128]{1,0:T(8,128)(2,1)} %curve.1, f32[256,128]{1,0:T(8,128)} %corr.3, f32[1,128]{1,0:T(1,128)} %bitcast.5, s32[1,128]{1,0:T(1,128)} %bitcast.6), custom_call_target="tpu_custom_call" | custom-call | tf_op jit(solution)/shard_map/pallas_call | solution.py:197
  1.8 2.0 %collective-permute-start = (bf16[1440,128]{1,0:T(8,128)(2,1)S(1)}, bf16[1440,128]{1,0:T(8,128)(2,1)S(1)}, u32[]{:S(2)}, u32[]{:S(2)}) collective-permute-start(bf16[1440,128]{1,0:T(8,128)(2,1)S(1)} %shard_map.114.mine), channel_id=1, source_target_pairs={{0,1},{1,0},{2,3},{3,2},{4,5},{5,4},{6,7},{7,6},{8,9},{9,8},{10,11... | collective-permute-start | bytes 1105928 | tf_op jit(solution)/shard_map/ppermute | solution.py:263
  3.8 0.9 shard_map.113
  4.7 0.7 collective-permute-done.other
  5.4 0.5 shard_map.115
  5.9 0.7 collective-permute-start.1
  6.6 5.4 %collective-permute-start.2 = (f32[32,256]{1,0:T(8,128)S(1)}, f32[32,256]{1,0:T(8,128)S(1)}, u32[]{:S(2)}, u32[]{:S(2)}) collective-permute-start(f32[32,256]{1,0:T(8,128)S(1)} %get-tuple-element.26.high), channel_id=1, source_target_pairs={{0,8},{8,16},{16,24},{24,32},{32,40},{40,48},{48,56},{56,64},{64,7... | collective-permute-start | bytes 98312 | tf_op jit(solution)/shard_map/ppermute | solution.py:211
  12.0 1.3 %collective-permute-start.3 = (f32[32,256]{1,0:T(8,128)S(1)}, f32[32,256]{1,0:T(8,128)S(1)}, u32[]{:S(2)}, u32[]{:S(2)}) collective-permute-start(f32[32,256]{1,0:T(8,128)S(1)} %get-tuple-element.27), channel_id=1, source_target_pairs={{8,0},{9,1},{10,2},{11,3},{12,4},{13,5},{14,6},{15,7},{264,256},{2... | collective-permute-start | bytes 98312 | tf_op jit(solution)/shard_map/ppermute | solution.py:294
  13.3 0.3 collective-permute-done.2.above
  13.5 5.0 %collective-permute-done.3.start = f32[32,256]{1,0:T(8,128)S(1)} collective-permute-done((f32[32,256]{1,0:T(8,128)S(1)}, f32[32,256]{1,0:T(8,128)S(1)}, u32[]{:S(2)}, u32[]{:S(2)}) %collective-permute-start.3) | collective-permute-done | bytes 32800 | tf_op jit(solution)/shard_map/ppermute | solution.py:294
  18.6 2.5 %shard_map.116 = bf16[16,40,128]{2,1,0:T(8,128)(2,1)S(1)} custom-call(f32[32,256]{1,0:T(8,128)S(1)} %get-tuple-element.24.low, f32[96,256]{1,0:T(8,128)S(1)} %get-tuple-element.25.mid, f32[32,256]{1,0:T(8,128)S(1)} %get-tuple-element.26.high, f32[32,256]{1,0:T(8,128)S(1)} %collective-permute-done.2.above, f32[32,256]{1,0:T(8,128)S(1)} %collective-permute-done.1.below, ...), custom_call_target="tpu_custom_call" | custom-call | tf_op jit(solution)/shard_map/pallas_call | solution.py:197
  21.1 50.5 %all_to_all.5.got = bf16[16,40,128]{2,1,0:T(8,128)(2,1)S(1)} all-to-all(bf16[16,40,128]{2,1,0:T(8,128)(2,1)S(1)} %shard_map.116), channel_id=1, replica_groups={{240,242,244,246,248,250,252,254,0,2,4,6,8,10,12,14},{16,18,20,22,24,26..., dimensions={0} | all-to-all | bytes 327680 | tf_op jit(solution)/shard_map/all_to_all | solution.py:222
  71.6 0.7 collective-permute-start.4
  72.3 0.7 collective-permute-start.5
  73.0 0.7 collective-permute-start.6
  73.7 1.3 %collective-permute-start.7 = (bf16[40,128]{1,0:T(8,128)(2,1)S(1)}, bf16[40,128]{1,0:T(8,128)(2,1)S(1)}, u32[]{:S(2)}, u32[]{:S(2)}) collective-permute-start(bf16[40,128]{1,0:T(8,128)(2,1)S(1)} %fusion.1), channel_id=1, source_target_pairs={{208,240},{216,248},{224,0},{232,8},{209,241},{217,249},{225,1},{2... | collective-permute-start | bytes 30728 | tf_op jit(solution)/shard_map/ppermute | solution.py:229
  75.0 1.3 %collective-permute-start.8 = (bf16[40,128]{1,0:T(8,128)(2,1)S(1)}, bf16[40,128]{1,0:T(8,128)(2,1)S(1)}, u32[]{:S(2)}, u32[]{:S(2)}) collective-permute-start(bf16[40,128]{1,0:T(8,128)(2,1)S(1)} %fusion.1), channel_id=1, source_target_pairs={{16,240},{24,248},{32,0},{40,8},{17,241},{25,249},{33,1},{41,9},{1... | collective-permute-start | bytes 30728 | tf_op jit(solution)/shard_map/ppermute | solution.py:229
  76.3 12.3 %collective-permute-done.7 = bf16[40,128]{1,0:T(8,128)(2,1)S(1)} collective-permute-done((bf16[40,128]{1,0:T(8,128)(2,1)S(1)}, bf16[40,128]{1,0:T(8,128)(2,1)S(1)}, u32[]{:S(2)}, u32[]{:S(2)}) %collective-permute-start.7) | collective-permute-done | bytes 10272 | tf_op jit(solution)/shard_map/ppermute | solution.py:229
  88.7 1.3 %collective-permute-start.10 = (bf16[40,128]{1,0:T(8,128)(2,1)S(1)}, bf16[40,128]{1,0:T(8,128)(2,1)S(1)}, u32[]{:S(2)}, u32[]{:S(2)}) collective-permute-start(bf16[40,128]{1,0:T(8,128)(2,1)S(1)} %add_convert_fusion.whole), channel_id=1, source_target_pairs={{8,16},{0,24},{248,32},{240,40},{9,17},{1,25},{249,33},{241,41},{1... | collective-permute-start | bytes 30728 | tf_op jit(solution)/shard_map/ppermute | solution.py:229
  90.0 1.3 %collective-permute-start.9 = (bf16[40,128]{1,0:T(8,128)(2,1)S(1)}, bf16[40,128]{1,0:T(8,128)(2,1)S(1)}, u32[]{:S(2)}, u32[]{:S(2)}) collective-permute-start(bf16[40,128]{1,0:T(8,128)(2,1)S(1)} %add_convert_fusion.whole), channel_id=1, source_target_pairs={{8,48},{0,56},{248,64},{240,72},{9,49},{1,57},{249,65},{241,73},{1... | collective-permute-start | bytes 30728 | tf_op jit(solution)/shard_map/ppermute | solution.py:229
  91.3 1.3 %collective-permute-done.9.second = bf16[40,128]{1,0:T(8,128)(2,1)S(1)} collective-permute-done((bf16[40,128]{1,0:T(8,128)(2,1)S(1)}, bf16[40,128]{1,0:T(8,128)(2,1)S(1)}, u32[]{:S(2)}, u32[]{:S(2)}) %collective-permute-start.9) | collective-permute-done | bytes 10272 | tf_op jit(solution)/shard_map/ppermute | solution.py:229
  92.7 0.7 collective-permute-start.11
  93.3 0.7 collective-permute-start.12
  94.0 0.6 shard_map.118
  (25 shorter events, 0.1 us)
Async XLA Ops:
  0.6 3.1 %copy-start = (f32[256,128]{1,0:T(8,128)S(1)}, f32[256,128]{1,0:T(8,128)}, u32[]{:S(2)}) copy-start(f32[256,128]{1,0:T(8,128)} %corr.3) | copy-start | bytes 393220
  0.6 3.1 %copy-start.1 = (bf16[512,256]{1,0:T(8,128)(2,1)S(1)}, bf16[512,256]{1,0:T(8,128)(2,1)}, u32[]{:S(2)}) copy-start(bf16[512,256]{1,0:T(8,128)(2,1)} %direction.1) | copy-start | bytes 786436
  0.7 3.1 %copy-start.2 = (bf16[32,256]{1,0:T(8,128)(2,1)S(1)}, bf16[32,256]{1,0:T(8,128)(2,1)}, u32[]{:S(2)}) copy-start(bf16[32,256]{1,0:T(8,128)(2,1)} %state.1) | copy-start | bytes 49156
  0.7 3.1 %copy-start.3 = (f32[32,128]{1,0:T(8,128)S(1)}, f32[32,128]{1,0:T(8,128)}, u32[]{:S(2)}) copy-start(f32[32,128]{1,0:T(8,128)} %funding.1) | copy-start | bytes 49156
  0.7 3.1 %copy-start.4 = (s32[512]{0:T(512)S(1)}, s32[512]{0:T(512)}, u32[]{:S(2)}) copy-start(s32[512]{0:T(512)} %param.14) | copy-start | bytes 6148
  1.8 3.6 %collective-permute-start = (bf16[1440,128]{1,0:T(8,128)(2,1)S(1)}, bf16[1440,128]{1,0:T(8,128)(2,1)S(1)}, u32[]{:S(2)}, u32[]{:S(2)}) collective-permute-start(bf16[1440,128]{1,0:T(8,128)(2,1)S(1)} %shard_map.114.mine), channel_id=1, source_target_pairs={{0,1},{1,0},{2,3},{3,2},{4,5},{5,4},{6,7},{7,6},{8,9},{9,8},{10,11... | collective-permute-start | bytes 1105928 | tf_op jit(solution)/shard_map/ppermute | solution.py:263
  5.9 7.4 %collective-permute-start.1 = (f32[32,256]{1,0:T(8,128)S(1)}, f32[32,256]{1,0:T(8,128)S(1)}, u32[]{:S(2)}, u32[]{:S(2)}) collective-permute-start(f32[32,256]{1,0:T(8,128)S(1)} %get-tuple-element.24.low), channel_id=1, source_target_pairs={{16,8},{24,16},{32,24},{40,32},{48,40},{56,48},{64,56},{72,64},{80... | collective-permute-start | bytes 98312 | tf_op jit(solution)/shard_map/ppermute | solution.py:211
  6.6 6.9 %collective-permute-start.2 = (f32[32,256]{1,0:T(8,128)S(1)}, f32[32,256]{1,0:T(8,128)S(1)}, u32[]{:S(2)}, u32[]{:S(2)}) collective-permute-start(f32[32,256]{1,0:T(8,128)S(1)} %get-tuple-element.26.high), channel_id=1, source_target_pairs={{0,8},{8,16},{16,24},{24,32},{32,40},{40,48},{48,56},{56,64},{64,7... | collective-permute-start | bytes 98312 | tf_op jit(solution)/shard_map/ppermute | solution.py:211
  12.0 6.6 %collective-permute-start.3 = (f32[32,256]{1,0:T(8,128)S(1)}, f32[32,256]{1,0:T(8,128)S(1)}, u32[]{:S(2)}, u32[]{:S(2)}) collective-permute-start(f32[32,256]{1,0:T(8,128)S(1)} %get-tuple-element.27), channel_id=1, source_target_pairs={{8,0},{9,1},{10,2},{11,3},{12,4},{13,5},{14,6},{15,7},{264,256},{2... | collective-permute-start | bytes 98312 | tf_op jit(solution)/shard_map/ppermute | solution.py:294
  71.6 1.3 %collective-permute-start.4 = (bf16[40,128]{1,0:T(8,128)(2,1)S(1)}, bf16[40,128]{1,0:T(8,128)(2,1)S(1)}, u32[]{:S(2)}, u32[]{:S(2)}) collective-permute-start(bf16[40,128]{1,0:T(8,128)(2,1)S(1)} %convert_element_type.29), channel_id=1, source_target_pairs={{176,208},{184,216},{192,224},{200,232},{112,80},{120,88},{128,96}... | collective-permute-start | bytes 30728 | tf_op jit(solution)/shard_map/ppermute | solution.py:229
  72.3 1.4 %collective-permute-start.5 = (bf16[40,128]{1,0:T(8,128)(2,1)S(1)}, bf16[40,128]{1,0:T(8,128)(2,1)S(1)}, u32[]{:S(2)}, u32[]{:S(2)}) collective-permute-start(bf16[40,128]{1,0:T(8,128)(2,1)S(1)} %convert_element_type.29), channel_id=1, source_target_pairs={{144,16},{152,24},{160,32},{168,40},{145,17},{153,25},{161,33},{16... | collective-permute-start | bytes 30728 | tf_op jit(solution)/shard_map/ppermute | solution.py:229
  73.0 0.7 collective-permute-start.6
  73.7 14.9 %collective-permute-start.7 = (bf16[40,128]{1,0:T(8,128)(2,1)S(1)}, bf16[40,128]{1,0:T(8,128)(2,1)S(1)}, u32[]{:S(2)}, u32[]{:S(2)}) collective-permute-start(bf16[40,128]{1,0:T(8,128)(2,1)S(1)} %fusion.1), channel_id=1, source_target_pairs={{208,240},{216,248},{224,0},{232,8},{209,241},{217,249},{225,1},{2... | collective-permute-start | bytes 30728 | tf_op jit(solution)/shard_map/ppermute | solution.py:229
  75.0 13.6 %collective-permute-start.8 = (bf16[40,128]{1,0:T(8,128)(2,1)S(1)}, bf16[40,128]{1,0:T(8,128)(2,1)S(1)}, u32[]{:S(2)}, u32[]{:S(2)}) collective-permute-start(bf16[40,128]{1,0:T(8,128)(2,1)S(1)} %fusion.1), channel_id=1, source_target_pairs={{16,240},{24,248},{32,0},{40,8},{17,241},{25,249},{33,1},{41,9},{1... | collective-permute-start | bytes 30728 | tf_op jit(solution)/shard_map/ppermute | solution.py:229
  88.7 2.7 %collective-permute-start.10 = (bf16[40,128]{1,0:T(8,128)(2,1)S(1)}, bf16[40,128]{1,0:T(8,128)(2,1)S(1)}, u32[]{:S(2)}, u32[]{:S(2)}) collective-permute-start(bf16[40,128]{1,0:T(8,128)(2,1)S(1)} %add_convert_fusion.whole), channel_id=1, source_target_pairs={{8,16},{0,24},{248,32},{240,40},{9,17},{1,25},{249,33},{241,41},{1... | collective-permute-start | bytes 30728 | tf_op jit(solution)/shard_map/ppermute | solution.py:229
  90.0 2.7 %collective-permute-start.9 = (bf16[40,128]{1,0:T(8,128)(2,1)S(1)}, bf16[40,128]{1,0:T(8,128)(2,1)S(1)}, u32[]{:S(2)}, u32[]{:S(2)}) collective-permute-start(bf16[40,128]{1,0:T(8,128)(2,1)S(1)} %add_convert_fusion.whole), channel_id=1, source_target_pairs={{8,48},{0,56},{248,64},{240,72},{9,49},{1,57},{249,65},{241,73},{1... | collective-permute-start | bytes 30728 | tf_op jit(solution)/shard_map/ppermute | solution.py:229
  92.7 0.7 collective-permute-start.11
  93.3 0.7 collective-permute-start.12

commit v6 on v5

--- a/solution.py
+++ b/solution.py
@@ -60,7 +60,11 @@
     pair_out[:, trades:] = money.astype(BF16)
     side = pl.multiple_of(lax.axis_index("fact") * half, half)
     side_out[...] = direction[:, pl.ds(side, half)]
-    corr_out[...] = corr[...]
+    far_side = pl.multiple_of((1 - lax.axis_index("fact")) * half, half)
+    cross = corr[pl.ds(far_side, half)]
+    corr_out[:half, :half] = corr[pl.ds(side, half)]
+    corr_out[half:, :half] = cross
+    corr_out[:half, half:] = cross.T
     first = lax.axis_index("trades") * NSET_DEV - 1
     place = jnp.broadcast_to(sets[...] - first, (8, trades))
     where_out[:, :trades] = place
@@ -73,7 +77,7 @@
     limit_out[...] = limit
 
 
-def window_kernel(pair, where, mine, other, low_out, mid_out, high_out, edge_out):
+def window_kernel(pair, where, mine, other, net_out, low_out, high_out, edge_out):
     scen, double = pair.shape
     paired = pair[...]
     place = where[:1]
@@ -81,26 +85,31 @@
     for w in range(SPAN):
         member = jnp.where(place == w, 1.0, 0.0).astype(BF16)
         mixing = paired * member
-        if w == 0:
-            out, at = low_out, 0
-        elif w < SPAN - 1:
-            out, at = mid_out, (w - 1) * scen
-        else:
-            out, at = high_out, 0
-        out[at : at + scen, :half] = dot(mixing, mine[:double])
-        out[at : at + scen, half:] = dot(mixing, other[:double])
-    edge_out[...] = low_out[...]
+        own = dot(mixing, mine[:double])
+        swapped = dot(mixing, other[:double])
+        net_out[w * scen : (w + 1) * scen, :half] = own
+        net_out[w * scen : (w + 1) * scen, half:] = swapped
+        for out in {0: (low_out, edge_out), SPAN - 1: (high_out,)}.get(w, ()):
+            out[:, :half] = own
+            out[:, half:] = swapped
+
+
+def sum_hot(x, hot, back=False):
+    product = dot if back else dot_t
+    high, mid, low = three_parts(x)
+    return product(high, hot) + product(mid, hot) + product(low, hot)
 
 
 def sets_kernel(
-    low, mid, high, above, below, start, mine, other, corr, fund, limits, where, money, side_of, out
+    net, above, below, start, mine, other, corr, fund, limits, where, money, side_of, out
 ):
-    scen, factors = low.shape
+    scen, factors = above.shape
     half = factors // 2
     double = mine.shape[0] - 3 * half - 32
-    side = pl.multiple_of(lax.axis_index("fact") * half, half)
-    far_side = pl.multiple_of((1 - lax.axis_index("fact")) * half, half)
-    netted = jnp.concatenate([low[...] + above[...], mid[...], high[...] + (below[...] + start[...])], axis=0)
+    last = (SPAN - 1) * scen
+    before = above[...]
+    after = below[...] + start[...]
+    netted = jnp.concatenate([net[:scen] + before, net[scen:last], net[last:] + after], axis=0)
     base = double + 3 * half
 
     def risk_of(ref):
@@ -113,24 +122,18 @@
     bucket = jnp.concatenate([bucket_of(mine), bucket_of(other)], axis=1).astype(jnp.int32)
     hot = jnp.where(
         lax.broadcasted_iota(jnp.int32, (16, factors), 0) == bucket, 1.0, 0.0
-    ).astype(F32)
+    ).astype(BF16)
     limit = limits[:1, :16]
-    bucket_sum = dot_t(netted, hot, precision=PRECISE)
+    bucket_sum = sum_hot(netted, hot)
     raw_ratio = jnp.sqrt(jnp.abs(bucket_sum) / limit)
     concentration = jnp.maximum(1.0, raw_ratio)
-    conc_factor = dot(concentration, hot, precision=PRECISE)
+    conc_factor = sum_hot(concentration, hot, back=True)
     scaled = risk * conc_factor
     weighted = scaled * netted
-    near_cols = corr[pl.ds(side, half)]
-    cross = corr[pl.ds(far_side, half)]
     far_cols = from_parts(*[other[double + i * half : double + (i + 1) * half] for i in range(3)])
-    w_own, w_far = weighted[:, :half], weighted[:, half:]
-    image = jnp.concatenate(
-        [
-            dot(w_own, near_cols, precision=PRECISE) + dot(w_far, cross, precision=PRECISE),
-            dot_t(w_own, cross, precision=PRECISE) + dot(w_far, far_cols, precision=PRECISE),
-        ],
-        axis=1,
+    far_rows = jnp.concatenate([corr[half:, :half], far_cols], axis=1)
+    image = dot(weighted[:, :half], corr[:half], precision=PRECISE) + dot(
+        weighted[:, half:], far_rows, precision=PRECISE
     )
     margin = jnp.sqrt(jnp.sum(weighted * image, axis=1, keepdims=True) + 1e-06)
     first = lax.axis_index("trades") * NSET_DEV - 1
@@ -144,10 +147,10 @@
         axis=0,
     )
     weighted_bar = (cost / margin) * image
-    conc_bar = dot_t(weighted_bar * risk * netted, hot, precision=PRECISE)
+    conc_bar = sum_hot(weighted_bar * risk * netted, hot)
     sign = jnp.where(bucket_sum > 0.0, 1.0, jnp.where(bucket_sum < 0.0, -1.0, 0.0))
     bucket_bar = jnp.where(raw_ratio > 1.0, conc_bar * sign / (2.0 * limit * concentration), 0.0)
-    bar = (weighted_bar * scaled + dot(bucket_bar, hot, precision=PRECISE)).astype(BF16)
+    bar = (weighted_bar * scaled + sum_hot(bucket_bar, hot, back=True)).astype(BF16)
     grad = weighted_bar[scen:, :half] * netted[scen:, :half] * conc_factor[scen:, :half]
     weight = jnp.broadcast_to(jnp.sum(grad, axis=0, keepdims=True), (8, half)).astype(BF16)
     trades = side_of.shape[0]
@@ -179,12 +182,12 @@
     total_out[scen:] = weight
 
 
-def last_kernel(count, whole, first, second, third, fourth, state_out, weight_out):
+def last_kernel(count, whole, first, second, third, fourth, fifth, state_out, weight_out):
     scen = state_out.shape[0]
     devs = lax.axis_size("trades")
     late = lax.rem(lax.axis_index("trades") + NEAR // 2, devs) < NEAR
-    parts = [x[...].astype(F32) for x in (whole, first, second, third, fourth)]
-    total = jnp.where(late, parts[0], parts[1] + parts[2] + parts[3] + parts[4])
+    parts = [x[...].astype(F32) for x in (first, second, third, fourth, fifth)]
+    total = jnp.where(late, whole[...].astype(F32), sum(parts[1:], parts[0]))
     state_out[...] = total[:scen]
     weight_out[...] = total[scen : scen + 1] * (1.0 / count)
 
@@ -230,13 +233,17 @@
 
     far = send(total, (5, 1, 0))
     total = total + send(total, (6, 7, 0), (4, 3, 0), (2, 1, 0)).astype(F32)
-    total = total + far.astype(F32) + send(total, (3, 1, 0)).astype(F32)
-    one, two = lax.optimization_barrier((send(total, (7, 0, 0)), send(total, (1, 0, 0))))
+    one = send(total, (7, 0, 0))
+    near = send(total, (3, 1, 0))
+    added = total + far.astype(F32) + near.astype(F32)
+    two = send(added, (1, 0, 0))
     whole = (total + one.astype(F32) + two.astype(F32)).astype(BF16)
-    second, first = lax.optimization_barrier((send(whole, (0, 2, 1)), send(whole, (0, 1, 1))))
-    third = send(jnp.where(mine == 1, first, second), (1, 3, 0), (2, 5, 0))
-    fourth = send(jnp.where(mine == 2, second, third), (3, 4, 0), (5, 6, 0), (2, 7, 0))
-    return whole, first, second, third, fourth
+    first = send(whole, (0, 1, 1))
+    second = send(whole, (0, 2, 1))
+    third = send(first, (1, 3, 0))
+    fourth = send(jnp.where(mine == 2, second, third), (3, 4, 0), (2, 5, 0))
+    fifth = send(fourth, (4, 7, 0), (5, 6, 0))
+    return whole, first, second, third, fourth, fifth
 
 
 def on_device(
@@ -267,7 +274,7 @@
             pltpu.VMEM((scen, trades), F32),
             pltpu.VMEM((scen, double), BF16),
             pltpu.VMEM((trades, half), BF16),
-            pltpu.VMEM((factors, half), F32),
+            pltpu.VMEM((factors, factors), F32),
             pltpu.VMEM((8, double), jnp.int32),
             pltpu.VMEM(funding.shape, F32),
             pltpu.VMEM((8, 128), F32),
@@ -280,11 +287,11 @@
     money, pair, side, corr, where, fund, limit = map(
         near_vmem, (money, pair, side, corr, where, fund, limit)
     )
-    low, mid, high, edge = call(
+    net, low, high, edge = call(
         window_kernel,
         (
+            pltpu.VMEM((SPAN * scen, factors), F32),
             pltpu.VMEM((scen, factors), F32),
-            pltpu.VMEM(((SPAN - 2) * scen, factors), F32),
             pltpu.VMEM((scen, factors), F32),
             pltpu.VMEM((scen, factors), F32),
         ),
@@ -294,11 +301,10 @@
         (shifted(low, "trades", -1, 2), shifted(high, "trades", 1), lax.ppermute(edge, "trades", [(1, 0)]))
     )
     below, above, start = near_vmem(below), near_vmem(above), near_vmem(start)
-    low, mid, high = near_vmem(low), near_vmem(mid), near_vmem(high)
     copies = call(
         sets_kernel,
         pltpu.VMEM((NEAR * lax.axis_size("scen"), scen + 8, half), BF16),
-        low, mid, high, above, below, start, mine, other, corr, fund, limit, where, money, side,
+        near_vmem(net), above, below, start, mine, other, corr, fund, limit, where, money, side,
     )
     count = scen * lax.axis_size("scen") * set_count
     state_grad, weight_grad = call(

time: 95 us -> 94.6 us (level)
    ppermute x9 -> x10, waiting for transfers between devices: 13.7 us -> 13 us  [send(): return lax.ppermute(x.astype(BF16), 'trades', pairs)]
    ppermute x9 -> x10, starting transfers between devices: 8.52 us -> 9.19 us  [send(): return lax.ppermute(x.astype(BF16), 'trades', pairs)]
  transfers between devices with their start and end apart: 13 -> 14, of which waited for: 5 -> 6; matrix products, arithmetic and copies ran while one was open for 0% -> 0% of each run, Pallas kernels for 1% -> 1%
where the time goes in v6:
time: 94.6 us; the launch traced here: 94.3 us
  blocking collectives  50.5 us (53%)
  waiting for transfers between devices  19 us (20%)
  starting transfers between devices  18.5 us (20%)
  Pallas kernels  5.29 us (6%)
  between operations  0.95 us (1%)
    all_to_all x1, blocking collectives, sum_over_trades(): lax.all_to_all(copies, ('trades', 'scen'), 0, 0, tiled=True, axis_index_g...  50.5 us
    ppermute x10, waiting for transfers between devices, send(): return lax.ppermute(x.astype(BF16), 'trades', pairs)  13 us
    ppermute x10, starting transfers between devices, send(): return lax.ppermute(x.astype(BF16), 'trades', pairs)  9.19 us
    ppermute x2, starting transfers between devices, shifted(): return lax.ppermute(x, axis, pairs)  6.02 us
    pallas_call x6, Pallas kernels, call(): pl.pallas_call(body, out_shape=out_shape, in_specs=[pl.BlockSpec(memory_s...  5.29 us
    ppermute x1, waiting for transfers between devices, on_device(): lax.ppermute(edge, 'trades', [(1, 0)])  5.03 us
    ppermute x1, starting transfers between devices, on_device(): other = lax.ppermute(mine, 'fact', [(0, 1), (1, 0)])  1.95 us
  transfers between devices with their start and end apart: 14, of which 6 were waited for; matrix products, arithmetic and copies ran while one was open for 0% of the time, Pallas kernels for 1%

profile of v6, /device:TPU:40, one launch (start us, length us, event | category | flops | bytes accessed | tf_op | source)
XLA Modules:
  0.0 94.3 jit_solution(4381403341871596306)
XLA Ops:
  0.7 1.1 %shard_map.114.mine = bf16[1440,128]{1,0:T(8,128)(2,1)S(1)} custom-call(bf16[512,128]{1,0:T(8,128)(2,1)} %load.1, bf16[512,128]{1,0:T(8,128)(2,1)} %curve.1, f32[256,128]{1,0:T(8,128)} %corr.3, f32[1,128]{1,0:T(1,128)} %bitcast.5, s32[1,128]{1,0:T(1,128)} %bitcast.6), custom_call_target="tpu_custom_call" | custom-call | tf_op jit(solution)/shard_map/pallas_call | solution.py:200
  1.8 2.0 %collective-permute-start = (bf16[1440,128]{1,0:T(8,128)(2,1)S(1)}, bf16[1440,128]{1,0:T(8,128)(2,1)S(1)}, u32[]{:S(2)}, u32[]{:S(2)}) collective-permute-start(bf16[1440,128]{1,0:T(8,128)(2,1)S(1)} %shard_map.114.mine), channel_id=1, source_target_pairs={{0,1},{1,0},{2,3},{3,2},{4,5},{5,4},{6,7},{7,6},{8,9},{9,8},{10,11... | collective-permute-start | bytes 1105928 | tf_op jit(solution)/shard_map/ppermute | solution.py:270
  3.8 0.9 shard_map.113
  4.7 0.7 collective-permute-done.other
  5.4 0.5 shard_map.115
  5.9 0.7 collective-permute-start.1
  6.6 5.4 %collective-permute-start.2 = (f32[32,256]{1,0:T(8,128)S(1)}, f32[32,256]{1,0:T(8,128)S(1)}, u32[]{:S(2)}, u32[]{:S(2)}) collective-permute-start(f32[32,256]{1,0:T(8,128)S(1)} %get-tuple-element.22), channel_id=1, source_target_pairs={{0,8},{8,16},{16,24},{24,32},{32,40},{40,48},{48,56},{56,64},{64,7... | collective-permute-start | bytes 98312 | tf_op jit(solution)/shard_map/ppermute | solution.py:214
  12.0 1.3 %collective-permute-start.3 = (f32[32,256]{1,0:T(8,128)S(1)}, f32[32,256]{1,0:T(8,128)S(1)}, u32[]{:S(2)}, u32[]{:S(2)}) collective-permute-start(f32[32,256]{1,0:T(8,128)S(1)} %get-tuple-element.23), channel_id=1, source_target_pairs={{8,0},{9,1},{10,2},{11,3},{12,4},{13,5},{14,6},{15,7},{264,256},{2... | collective-permute-start | bytes 98312 | tf_op jit(solution)/shard_map/ppermute | solution.py:301
  13.5 5.0 %collective-permute-done.3.start = f32[32,256]{1,0:T(8,128)S(1)} collective-permute-done((f32[32,256]{1,0:T(8,128)S(1)}, f32[32,256]{1,0:T(8,128)S(1)}, u32[]{:S(2)}, u32[]{:S(2)}) %collective-permute-start.3) | collective-permute-done | bytes 32800 | tf_op jit(solution)/shard_map/ppermute | solution.py:301
  18.6 2.2 %shard_map.116 = bf16[16,40,128]{2,1,0:T(8,128)(2,1)S(1)} custom-call(f32[160,256]{1,0:T(8,128)S(1)} %get-tuple-element.20.net, f32[32,256]{1,0:T(8,128)S(1)} %collective-permute-done.2.above, f32[32,256]{1,0:T(8,128)S(1)} %collective-permute-done.1.below, f32[32,256]{1,0:T(8,128)S(1)} %collective-permute-done.3.start, ...), custom_call_target="tpu_custom_call" | custom-call | tf_op jit(solution)/shard_map/pallas_call | solution.py:200
  20.7 50.5 %all_to_all.5.got = bf16[16,40,128]{2,1,0:T(8,128)(2,1)S(1)} all-to-all(bf16[16,40,128]{2,1,0:T(8,128)(2,1)S(1)} %shard_map.116), channel_id=1, replica_groups={{240,242,244,246,248,250,252,254,0,2,4,6,8,10,12,14},{16,18,20,22,24,26..., dimensions={0} | all-to-all | bytes 327680 | tf_op jit(solution)/shard_map/all_to_all | solution.py:225
  71.3 0.7 collective-permute-start.4
  71.9 0.7 collective-permute-start.6
  72.6 0.7 collective-permute-start.7
  73.3 1.3 %collective-permute-start.5 = (bf16[40,128]{1,0:T(8,128)(2,1)S(1)}, bf16[40,128]{1,0:T(8,128)(2,1)S(1)}, u32[]{:S(2)}, u32[]{:S(2)}) collective-permute-start(bf16[40,128]{1,0:T(8,128)(2,1)S(1)} %fusion), channel_id=1, source_target_pairs={{208,240},{216,248},{224,0},{232,8},{209,241},{217,249},{225,1},{2... | collective-permute-start | bytes 30728 | tf_op jit(solution)/shard_map/ppermute | solution.py:232
  74.7 1.3 %collective-permute-start.8 = (bf16[40,128]{1,0:T(8,128)(2,1)S(1)}, bf16[40,128]{1,0:T(8,128)(2,1)S(1)}, u32[]{:S(2)}, u32[]{:S(2)}) collective-permute-start(bf16[40,128]{1,0:T(8,128)(2,1)S(1)} %add_convert_fusion.1), channel_id=1, source_target_pairs={{16,240},{24,248},{32,0},{40,8},{17,241},{25,249},{33,1},{41,9},{1... | collective-permute-start | bytes 30728 | tf_op jit(solution)/shard_map/ppermute | solution.py:232
  76.0 12.3 %collective-permute-done.5 = bf16[40,128]{1,0:T(8,128)(2,1)S(1)} collective-permute-done((bf16[40,128]{1,0:T(8,128)(2,1)S(1)}, bf16[40,128]{1,0:T(8,128)(2,1)S(1)}, u32[]{:S(2)}, u32[]{:S(2)}) %collective-permute-start.5) | collective-permute-done | bytes 10272 | tf_op jit(solution)/shard_map/ppermute | solution.py:232
  88.3 1.3 %collective-permute-start.9 = (bf16[40,128]{1,0:T(8,128)(2,1)S(1)}, bf16[40,128]{1,0:T(8,128)(2,1)S(1)}, u32[]{:S(2)}, u32[]{:S(2)}) collective-permute-start(bf16[40,128]{1,0:T(8,128)(2,1)S(1)} %add_convert_fusion.whole), channel_id=1, source_target_pairs={{8,16},{0,24},{248,32},{240,40},{9,17},{1,25},{249,33},{241,41},{1... | collective-permute-start | bytes 30728 | tf_op jit(solution)/shard_map/ppermute | solution.py:232
  89.6 1.3 %collective-permute-start.10 = (bf16[40,128]{1,0:T(8,128)(2,1)S(1)}, bf16[40,128]{1,0:T(8,128)(2,1)S(1)}, u32[]{:S(2)}, u32[]{:S(2)}) collective-permute-start(bf16[40,128]{1,0:T(8,128)(2,1)S(1)} %add_convert_fusion.whole), channel_id=1, source_target_pairs={{8,48},{0,56},{248,64},{240,72},{9,49},{1,57},{249,65},{241,73},{1... | collective-permute-start | bytes 30728 | tf_op jit(solution)/shard_map/ppermute | solution.py:232
  90.9 0.7 collective-permute-start.11
  91.6 0.6 collective-permute-done.10.second
  92.3 0.7 collective-permute-start.12
  92.9 0.7 collective-permute-start.13
  93.6 0.6 shard_map.118
  (26 shorter events, 0.4 us)
Async XLA Ops:
  0.6 3.1 %copy-start = (f32[256,128]{1,0:T(8,128)S(1)}, f32[256,128]{1,0:T(8,128)}, u32[]{:S(2)}) copy-start(f32[256,128]{1,0:T(8,128)} %corr.3) | copy-start | bytes 393220
  0.6 3.1 %copy-start.1 = (bf16[512,256]{1,0:T(8,128)(2,1)S(1)}, bf16[512,256]{1,0:T(8,128)(2,1)}, u32[]{:S(2)}) copy-start(bf16[512,256]{1,0:T(8,128)(2,1)} %direction.1) | copy-start | bytes 786436
  0.7 3.1 %copy-start.2 = (bf16[32,256]{1,0:T(8,128)(2,1)S(1)}, bf16[32,256]{1,0:T(8,128)(2,1)}, u32[]{:S(2)}) copy-start(bf16[32,256]{1,0:T(8,128)(2,1)} %state.1) | copy-start | bytes 49156
  0.7 3.1 %copy-start.3 = (f32[32,128]{1,0:T(8,128)S(1)}, f32[32,128]{1,0:T(8,128)}, u32[]{:S(2)}) copy-start(f32[32,128]{1,0:T(8,128)} %funding.1) | copy-start | bytes 49156
  0.7 3.1 %copy-start.4 = (s32[512]{0:T(512)S(1)}, s32[512]{0:T(512)}, u32[]{:S(2)}) copy-start(s32[512]{0:T(512)} %param.14) | copy-start | bytes 6148
  1.8 3.6 %collective-permute-start = (bf16[1440,128]{1,0:T(8,128)(2,1)S(1)}, bf16[1440,128]{1,0:T(8,128)(2,1)S(1)}, u32[]{:S(2)}, u32[]{:S(2)}) collective-permute-start(bf16[1440,128]{1,0:T(8,128)(2,1)S(1)} %shard_map.114.mine), channel_id=1, source_target_pairs={{0,1},{1,0},{2,3},{3,2},{4,5},{5,4},{6,7},{7,6},{8,9},{9,8},{10,11... | collective-permute-start | bytes 1105928 | tf_op jit(solution)/shard_map/ppermute | solution.py:270
  5.9 7.4 %collective-permute-start.1 = (f32[32,256]{1,0:T(8,128)S(1)}, f32[32,256]{1,0:T(8,128)S(1)}, u32[]{:S(2)}, u32[]{:S(2)}) collective-permute-start(f32[32,256]{1,0:T(8,128)S(1)} %get-tuple-element.21), channel_id=1, source_target_pairs={{16,8},{24,16},{32,24},{40,32},{48,40},{56,48},{64,56},{72,64},{80... | collective-permute-start | bytes 98312 | tf_op jit(solution)/shard_map/ppermute | solution.py:214
  6.6 6.9 %collective-permute-start.2 = (f32[32,256]{1,0:T(8,128)S(1)}, f32[32,256]{1,0:T(8,128)S(1)}, u32[]{:S(2)}, u32[]{:S(2)}) collective-permute-start(f32[32,256]{1,0:T(8,128)S(1)} %get-tuple-element.22), channel_id=1, source_target_pairs={{0,8},{8,16},{16,24},{24,32},{32,40},{40,48},{48,56},{56,64},{64,7... | collective-permute-start | bytes 98312 | tf_op jit(solution)/shard_map/ppermute | solution.py:214
  12.0 6.6 %collective-permute-start.3 = (f32[32,256]{1,0:T(8,128)S(1)}, f32[32,256]{1,0:T(8,128)S(1)}, u32[]{:S(2)}, u32[]{:S(2)}) collective-permute-start(f32[32,256]{1,0:T(8,128)S(1)} %get-tuple-element.23), channel_id=1, source_target_pairs={{8,0},{9,1},{10,2},{11,3},{12,4},{13,5},{14,6},{15,7},{264,256},{2... | collective-permute-start | bytes 98312 | tf_op jit(solution)/shard_map/ppermute | solution.py:301
  71.3 1.3 %collective-permute-start.4 = (bf16[40,128]{1,0:T(8,128)(2,1)S(1)}, bf16[40,128]{1,0:T(8,128)(2,1)S(1)}, u32[]{:S(2)}, u32[]{:S(2)}) collective-permute-start(bf16[40,128]{1,0:T(8,128)(2,1)S(1)} %convert_element_type.29), channel_id=1, source_target_pairs={{176,208},{184,216},{192,224},{200,232},{112,80},{120,88},{128,96}... | collective-permute-start | bytes 30728 | tf_op jit(solution)/shard_map/ppermute | solution.py:232
  71.9 2.7 %collective-permute-start.6 = (bf16[40,128]{1,0:T(8,128)(2,1)S(1)}, bf16[40,128]{1,0:T(8,128)(2,1)S(1)}, u32[]{:S(2)}, u32[]{:S(2)}) collective-permute-start(bf16[40,128]{1,0:T(8,128)(2,1)S(1)} %convert_element_type.29), channel_id=1, source_target_pairs={{144,16},{152,24},{160,32},{168,40},{145,17},{153,25},{161,33},{16... | collective-permute-start | bytes 30728 | tf_op jit(solution)/shard_map/ppermute | solution.py:232
  72.6 2.0 %collective-permute-start.7 = (bf16[40,128]{1,0:T(8,128)(2,1)S(1)}, bf16[40,128]{1,0:T(8,128)(2,1)S(1)}, u32[]{:S(2)}, u32[]{:S(2)}) collective-permute-start(bf16[40,128]{1,0:T(8,128)(2,1)S(1)} %fusion), channel_id=1, source_target_pairs={{80,16},{88,24},{96,32},{104,40},{81,17},{89,25},{97,33},{105,41},... | collective-permute-start | bytes 30728 | tf_op jit(solution)/shard_map/ppermute | solution.py:232
  73.3 14.9 %collective-permute-start.5 = (bf16[40,128]{1,0:T(8,128)(2,1)S(1)}, bf16[40,128]{1,0:T(8,128)(2,1)S(1)}, u32[]{:S(2)}, u32[]{:S(2)}) collective-permute-start(bf16[40,128]{1,0:T(8,128)(2,1)S(1)} %fusion), channel_id=1, source_target_pairs={{208,240},{216,248},{224,0},{232,8},{209,241},{217,249},{225,1},{2... | collective-permute-start | bytes 30728 | tf_op jit(solution)/shard_map/ppermute | solution.py:232
  74.7 13.6 %collective-permute-start.8 = (bf16[40,128]{1,0:T(8,128)(2,1)S(1)}, bf16[40,128]{1,0:T(8,128)(2,1)S(1)}, u32[]{:S(2)}, u32[]{:S(2)}) collective-permute-start(bf16[40,128]{1,0:T(8,128)(2,1)S(1)} %add_convert_fusion.1), channel_id=1, source_target_pairs={{16,240},{24,248},{32,0},{40,8},{17,241},{25,249},{33,1},{41,9},{1... | collective-permute-start | bytes 30728 | tf_op jit(solution)/shard_map/ppermute | solution.py:232
  88.3 2.7 %collective-permute-start.9 = (bf16[40,128]{1,0:T(8,128)(2,1)S(1)}, bf16[40,128]{1,0:T(8,128)(2,1)S(1)}, u32[]{:S(2)}, u32[]{:S(2)}) collective-permute-start(bf16[40,128]{1,0:T(8,128)(2,1)S(1)} %add_convert_fusion.whole), channel_id=1, source_target_pairs={{8,16},{0,24},{248,32},{240,40},{9,17},{1,25},{249,33},{241,41},{1... | collective-permute-start | bytes 30728 | tf_op jit(solution)/shard_map/ppermute | solution.py:232
  89.6 2.7 %collective-permute-start.10 = (bf16[40,128]{1,0:T(8,128)(2,1)S(1)}, bf16[40,128]{1,0:T(8,128)(2,1)S(1)}, u32[]{:S(2)}, u32[]{:S(2)}) collective-permute-start(bf16[40,128]{1,0:T(8,128)(2,1)S(1)} %add_convert_fusion.whole), channel_id=1, source_target_pairs={{8,48},{0,56},{248,64},{240,72},{9,49},{1,57},{249,65},{241,73},{1... | collective-permute-start | bytes 30728 | tf_op jit(solution)/shard_map/ppermute | solution.py:232
  90.9 1.3 %collective-permute-start.11 = (bf16[40,128]{1,0:T(8,128)(2,1)S(1)}, bf16[40,128]{1,0:T(8,128)(2,1)S(1)}, u32[]{:S(2)}, u32[]{:S(2)}) collective-permute-start(bf16[40,128]{1,0:T(8,128)(2,1)S(1)} %collective-permute-done.9.first), channel_id=1, source_target_pairs={{16,80},{24,88},{32,96},{40,104},{17,81},{25,89},{33,97},{41,105},... | collective-permute-start | bytes 30728 | tf_op jit(solution)/shard_map/ppermute | solution.py:232
  92.3 0.7 collective-permute-start.12
  92.9 0.7 collective-permute-start.13

commit v7 on v6

--- a/solution.py
+++ b/solution.py
@@ -10,6 +10,7 @@
 NSET_DEV = 4
 SPAN = NSET_DEV + 1
 NEAR = 4
+MIRROR = (3, 2, 1, 0)
 F32 = jnp.float32
 BF16 = jnp.bfloat16
 PRECISE = lax.Precision.HIGHEST
@@ -228,18 +229,19 @@
     def send(x, *links):
         pairs = []
         for a, b, flip in links:
-            pairs += [(place(a, NEAR - 1 - j if flip else j), place(b, j)) for j in range(NEAR)]
+            order = flip or range(NEAR)
+            pairs += [(place(a, order[j]), place(b, j)) for j in range(NEAR)]
         return lax.ppermute(x.astype(BF16), "trades", pairs)
 
     far = send(total, (5, 1, 0))
     total = total + send(total, (6, 7, 0), (4, 3, 0), (2, 1, 0)).astype(F32)
-    one = send(total, (7, 0, 0))
+    one = send(total, (7, 0, (0, 1, 3, 2)))
     near = send(total, (3, 1, 0))
     added = total + far.astype(F32) + near.astype(F32)
-    two = send(added, (1, 0, 0))
+    two = send(added, (1, 0, (0, 2, 1, 3)))
     whole = (total + one.astype(F32) + two.astype(F32)).astype(BF16)
-    first = send(whole, (0, 1, 1))
-    second = send(whole, (0, 2, 1))
+    first = send(whole, (0, 1, MIRROR))
+    second = send(whole, (0, 2, MIRROR))
     third = send(first, (1, 3, 0))
     fourth = send(jnp.where(mine == 2, second, third), (3, 4, 0), (2, 5, 0))
     fifth = send(fourth, (4, 7, 0), (5, 6, 0))

time: 94.6 us -> 94.2 us (level)
  no operation moved by 1% of the time
where the time goes in v7:
time: 94.2 us; the launch traced here: 93.7 us
  blocking collectives  50.5 us (54%)
  starting transfers between devices  18.5 us (20%)
  waiting for transfers between devices  18.4 us (20%)
  Pallas kernels  5.29 us (6%)
  between operations  0.95 us (1%)
    all_to_all x1, blocking collectives, sum_over_trades(): lax.all_to_all(copies, ('trades', 'scen'), 0, 0, tiled=True, axis_index_g...  50.5 us
    ppermute x10, waiting for transfers between devices, send(): return lax.ppermute(x.astype(BF16), 'trades', pairs)  12.4 us
    ppermute x10, starting transfers between devices, send(): return lax.ppermute(x.astype(BF16), 'trades', pairs)  9.19 us
    ppermute x2, starting transfers between devices, shifted(): return lax.ppermute(x, axis, pairs)  6.02 us
    pallas_call x6, Pallas kernels, call(): pl.pallas_call(body, out_shape=out_shape, in_specs=[pl.BlockSpec(memory_s...  5.29 us
    ppermute x1, waiting for transfers between devices, on_device(): lax.ppermute(edge, 'trades', [(1, 0)])  5.03 us
    ppermute x1, starting transfers between devices, on_device(): other = lax.ppermute(mine, 'fact', [(0, 1), (1, 0)])  1.95 us
  transfers between devices with their start and end apart: 14, of which 6 were waited for; matrix products, arithmetic and copies ran while one was open for 0% of the time, Pallas kernels for 1%

profile of v7, /device:TPU:40, one launch (start us, length us, event | category | flops | bytes accessed | tf_op | source)
XLA Modules:
  0.0 93.7 jit_solution(4435135861427243226)
XLA Ops:
  0.7 1.1 %shard_map.114.mine = bf16[1440,128]{1,0:T(8,128)(2,1)S(1)} custom-call(bf16[512,128]{1,0:T(8,128)(2,1)} %load.1, bf16[512,128]{1,0:T(8,128)(2,1)} %curve.1, f32[256,128]{1,0:T(8,128)} %corr.3, f32[1,128]{1,0:T(1,128)} %bitcast.5, s32[1,128]{1,0:T(1,128)} %bitcast.6), custom_call_target="tpu_custom_call" | custom-call | tf_op jit(solution)/shard_map/pallas_call | solution.py:201
  1.8 2.0 %collective-permute-start = (bf16[1440,128]{1,0:T(8,128)(2,1)S(1)}, bf16[1440,128]{1,0:T(8,128)(2,1)S(1)}, u32[]{:S(2)}, u32[]{:S(2)}) collective-permute-start(bf16[1440,128]{1,0:T(8,128)(2,1)S(1)} %shard_map.114.mine), channel_id=1, source_target_pairs={{0,1},{1,0},{2,3},{3,2},{4,5},{5,4},{6,7},{7,6},{8,9},{9,8},{10,11... | collective-permute-start | bytes 1105928 | tf_op jit(solution)/shard_map/ppermute | solution.py:272
  3.8 0.9 shard_map.113
  4.7 0.7 collective-permute-done.other
  5.4 0.5 shard_map.115
  5.9 0.7 collective-permute-start.1
  6.6 5.4 %collective-permute-start.2 = (f32[32,256]{1,0:T(8,128)S(1)}, f32[32,256]{1,0:T(8,128)S(1)}, u32[]{:S(2)}, u32[]{:S(2)}) collective-permute-start(f32[32,256]{1,0:T(8,128)S(1)} %get-tuple-element.22), channel_id=1, source_target_pairs={{0,8},{8,16},{16,24},{24,32},{32,40},{40,48},{48,56},{56,64},{64,7... | collective-permute-start | bytes 98312 | tf_op jit(solution)/shard_map/ppermute | solution.py:215
  12.0 1.3 %collective-permute-start.3 = (f32[32,256]{1,0:T(8,128)S(1)}, f32[32,256]{1,0:T(8,128)S(1)}, u32[]{:S(2)}, u32[]{:S(2)}) collective-permute-start(f32[32,256]{1,0:T(8,128)S(1)} %get-tuple-element.23), channel_id=1, source_target_pairs={{8,0},{9,1},{10,2},{11,3},{12,4},{13,5},{14,6},{15,7},{264,256},{2... | collective-permute-start | bytes 98312 | tf_op jit(solution)/shard_map/ppermute | solution.py:303
  13.5 5.0 %collective-permute-done.3.start = f32[32,256]{1,0:T(8,128)S(1)} collective-permute-done((f32[32,256]{1,0:T(8,128)S(1)}, f32[32,256]{1,0:T(8,128)S(1)}, u32[]{:S(2)}, u32[]{:S(2)}) %collective-permute-start.3) | collective-permute-done | bytes 32800 | tf_op jit(solution)/shard_map/ppermute | solution.py:303
  18.6 2.2 %shard_map.116 = bf16[16,40,128]{2,1,0:T(8,128)(2,1)S(1)} custom-call(f32[160,256]{1,0:T(8,128)S(1)} %get-tuple-element.20.net, f32[32,256]{1,0:T(8,128)S(1)} %collective-permute-done.2.above, f32[32,256]{1,0:T(8,128)S(1)} %collective-permute-done.1.below, f32[32,256]{1,0:T(8,128)S(1)} %collective-permute-done.3.start, ...), custom_call_target="tpu_custom_call" | custom-call | tf_op jit(solution)/shard_map/pallas_call | solution.py:201
  20.7 50.5 %all_to_all.5.got = bf16[16,40,128]{2,1,0:T(8,128)(2,1)S(1)} all-to-all(bf16[16,40,128]{2,1,0:T(8,128)(2,1)S(1)} %shard_map.116), channel_id=1, replica_groups={{240,242,244,246,248,250,252,254,0,2,4,6,8,10,12,14},{16,18,20,22,24,26..., dimensions={0} | all-to-all | bytes 327680 | tf_op jit(solution)/shard_map/all_to_all | solution.py:226
  71.3 0.7 collective-permute-start.4
  71.9 0.7 collective-permute-start.6
  72.6 0.7 collective-permute-start.7
  73.3 1.3 %collective-permute-start.5 = (bf16[40,128]{1,0:T(8,128)(2,1)S(1)}, bf16[40,128]{1,0:T(8,128)(2,1)S(1)}, u32[]{:S(2)}, u32[]{:S(2)}) collective-permute-start(bf16[40,128]{1,0:T(8,128)(2,1)S(1)} %fusion), channel_id=1, source_target_pairs={{208,240},{216,248},{232,0},{224,8},{209,241},{217,249},{233,1},{2... | collective-permute-start | bytes 30728 | tf_op jit(solution)/shard_map/ppermute | solution.py:234
  74.7 1.3 %collective-permute-start.8 = (bf16[40,128]{1,0:T(8,128)(2,1)S(1)}, bf16[40,128]{1,0:T(8,128)(2,1)S(1)}, u32[]{:S(2)}, u32[]{:S(2)}) collective-permute-start(bf16[40,128]{1,0:T(8,128)(2,1)S(1)} %add_convert_fusion.1), channel_id=1, source_target_pairs={{16,240},{32,248},{24,0},{40,8},{17,241},{33,249},{25,1},{41,9},{1... | collective-permute-start | bytes 30728 | tf_op jit(solution)/shard_map/ppermute | solution.py:234
  76.0 11.7 %collective-permute-done.5 = bf16[40,128]{1,0:T(8,128)(2,1)S(1)} collective-permute-done((bf16[40,128]{1,0:T(8,128)(2,1)S(1)}, bf16[40,128]{1,0:T(8,128)(2,1)S(1)}, u32[]{:S(2)}, u32[]{:S(2)}) %collective-permute-start.5) | collective-permute-done | bytes 10272 | tf_op jit(solution)/shard_map/ppermute | solution.py:234
  87.7 1.3 %collective-permute-start.9 = (bf16[40,128]{1,0:T(8,128)(2,1)S(1)}, bf16[40,128]{1,0:T(8,128)(2,1)S(1)}, u32[]{:S(2)}, u32[]{:S(2)}) collective-permute-start(bf16[40,128]{1,0:T(8,128)(2,1)S(1)} %add_convert_fusion.whole), channel_id=1, source_target_pairs={{8,16},{0,24},{248,32},{240,40},{9,17},{1,25},{249,33},{241,41},{1... | collective-permute-start | bytes 30728 | tf_op jit(solution)/shard_map/ppermute | solution.py:234
  89.0 1.3 %collective-permute-start.10 = (bf16[40,128]{1,0:T(8,128)(2,1)S(1)}, bf16[40,128]{1,0:T(8,128)(2,1)S(1)}, u32[]{:S(2)}, u32[]{:S(2)}) collective-permute-start(bf16[40,128]{1,0:T(8,128)(2,1)S(1)} %add_convert_fusion.whole), channel_id=1, source_target_pairs={{8,48},{0,56},{248,64},{240,72},{9,49},{1,57},{249,65},{241,73},{1... | collective-permute-start | bytes 30728 | tf_op jit(solution)/shard_map/ppermute | solution.py:234
  90.4 0.7 collective-permute-start.11
  91.1 0.6 collective-permute-done.10.second
  91.7 0.7 collective-permute-start.12
  92.4 0.7 collective-permute-start.13
  93.1 0.6 shard_map.118
  (26 shorter events, 0.4 us)
Async XLA Ops:
  0.6 3.1 %copy-start = (f32[256,128]{1,0:T(8,128)S(1)}, f32[256,128]{1,0:T(8,128)}, u32[]{:S(2)}) copy-start(f32[256,128]{1,0:T(8,128)} %corr.3) | copy-start | bytes 393220
  0.6 3.1 %copy-start.1 = (bf16[512,256]{1,0:T(8,128)(2,1)S(1)}, bf16[512,256]{1,0:T(8,128)(2,1)}, u32[]{:S(2)}) copy-start(bf16[512,256]{1,0:T(8,128)(2,1)} %direction.1) | copy-start | bytes 786436
  0.7 3.1 %copy-start.2 = (bf16[32,256]{1,0:T(8,128)(2,1)S(1)}, bf16[32,256]{1,0:T(8,128)(2,1)}, u32[]{:S(2)}) copy-start(bf16[32,256]{1,0:T(8,128)(2,1)} %state.1) | copy-start | bytes 49156
  0.7 3.1 %copy-start.3 = (f32[32,128]{1,0:T(8,128)S(1)}, f32[32,128]{1,0:T(8,128)}, u32[]{:S(2)}) copy-start(f32[32,128]{1,0:T(8,128)} %funding.1) | copy-start | bytes 49156
  0.7 3.1 %copy-start.4 = (s32[512]{0:T(512)S(1)}, s32[512]{0:T(512)}, u32[]{:S(2)}) copy-start(s32[512]{0:T(512)} %param.14) | copy-start | bytes 6148
  1.8 3.6 %collective-permute-start = (bf16[1440,128]{1,0:T(8,128)(2,1)S(1)}, bf16[1440,128]{1,0:T(8,128)(2,1)S(1)}, u32[]{:S(2)}, u32[]{:S(2)}) collective-permute-start(bf16[1440,128]{1,0:T(8,128)(2,1)S(1)} %shard_map.114.mine), channel_id=1, source_target_pairs={{0,1},{1,0},{2,3},{3,2},{4,5},{5,4},{6,7},{7,6},{8,9},{9,8},{10,11... | collective-permute-start | bytes 1105928 | tf_op jit(solution)/shard_map/ppermute | solution.py:272
  5.9 7.4 %collective-permute-start.1 = (f32[32,256]{1,0:T(8,128)S(1)}, f32[32,256]{1,0:T(8,128)S(1)}, u32[]{:S(2)}, u32[]{:S(2)}) collective-permute-start(f32[32,256]{1,0:T(8,128)S(1)} %get-tuple-element.21), channel_id=1, source_target_pairs={{16,8},{24,16},{32,24},{40,32},{48,40},{56,48},{64,56},{72,64},{80... | collective-permute-start | bytes 98312 | tf_op jit(solution)/shard_map/ppermute | solution.py:215
  6.6 6.9 %collective-permute-start.2 = (f32[32,256]{1,0:T(8,128)S(1)}, f32[32,256]{1,0:T(8,128)S(1)}, u32[]{:S(2)}, u32[]{:S(2)}) collective-permute-start(f32[32,256]{1,0:T(8,128)S(1)} %get-tuple-element.22), channel_id=1, source_target_pairs={{0,8},{8,16},{16,24},{24,32},{32,40},{40,48},{48,56},{56,64},{64,7... | collective-permute-start | bytes 98312 | tf_op jit(solution)/shard_map/ppermute | solution.py:215
  12.0 6.6 %collective-permute-start.3 = (f32[32,256]{1,0:T(8,128)S(1)}, f32[32,256]{1,0:T(8,128)S(1)}, u32[]{:S(2)}, u32[]{:S(2)}) collective-permute-start(f32[32,256]{1,0:T(8,128)S(1)} %get-tuple-element.23), channel_id=1, source_target_pairs={{8,0},{9,1},{10,2},{11,3},{12,4},{13,5},{14,6},{15,7},{264,256},{2... | collective-permute-start | bytes 98312 | tf_op jit(solution)/shard_map/ppermute | solution.py:303
  71.3 1.3 %collective-permute-start.4 = (bf16[40,128]{1,0:T(8,128)(2,1)S(1)}, bf16[40,128]{1,0:T(8,128)(2,1)S(1)}, u32[]{:S(2)}, u32[]{:S(2)}) collective-permute-start(bf16[40,128]{1,0:T(8,128)(2,1)S(1)} %convert_element_type.29), channel_id=1, source_target_pairs={{176,208},{184,216},{192,224},{200,232},{112,80},{120,88},{128,96}... | collective-permute-start | bytes 30728 | tf_op jit(solution)/shard_map/ppermute | solution.py:234
  71.9 2.7 %collective-permute-start.6 = (bf16[40,128]{1,0:T(8,128)(2,1)S(1)}, bf16[40,128]{1,0:T(8,128)(2,1)S(1)}, u32[]{:S(2)}, u32[]{:S(2)}) collective-permute-start(bf16[40,128]{1,0:T(8,128)(2,1)S(1)} %convert_element_type.29), channel_id=1, source_target_pairs={{144,16},{152,24},{160,32},{168,40},{145,17},{153,25},{161,33},{16... | collective-permute-start | bytes 30728 | tf_op jit(solution)/shard_map/ppermute | solution.py:234
  72.6 2.0 %collective-permute-start.7 = (bf16[40,128]{1,0:T(8,128)(2,1)S(1)}, bf16[40,128]{1,0:T(8,128)(2,1)S(1)}, u32[]{:S(2)}, u32[]{:S(2)}) collective-permute-start(bf16[40,128]{1,0:T(8,128)(2,1)S(1)} %fusion), channel_id=1, source_target_pairs={{80,16},{88,24},{96,32},{104,40},{81,17},{89,25},{97,33},{105,41},... | collective-permute-start | bytes 30728 | tf_op jit(solution)/shard_map/ppermute | solution.py:234
  73.3 14.4 %collective-permute-start.5 = (bf16[40,128]{1,0:T(8,128)(2,1)S(1)}, bf16[40,128]{1,0:T(8,128)(2,1)S(1)}, u32[]{:S(2)}, u32[]{:S(2)}) collective-permute-start(bf16[40,128]{1,0:T(8,128)(2,1)S(1)} %fusion), channel_id=1, source_target_pairs={{208,240},{216,248},{232,0},{224,8},{209,241},{217,249},{233,1},{2... | collective-permute-start | bytes 30728 | tf_op jit(solution)/shard_map/ppermute | solution.py:234
  74.7 13.0 %collective-permute-start.8 = (bf16[40,128]{1,0:T(8,128)(2,1)S(1)}, bf16[40,128]{1,0:T(8,128)(2,1)S(1)}, u32[]{:S(2)}, u32[]{:S(2)}) collective-permute-start(bf16[40,128]{1,0:T(8,128)(2,1)S(1)} %add_convert_fusion.1), channel_id=1, source_target_pairs={{16,240},{32,248},{24,0},{40,8},{17,241},{33,249},{25,1},{41,9},{1... | collective-permute-start | bytes 30728 | tf_op jit(solution)/shard_map/ppermute | solution.py:234
  87.7 2.7 %collective-permute-start.9 = (bf16[40,128]{1,0:T(8,128)(2,1)S(1)}, bf16[40,128]{1,0:T(8,128)(2,1)S(1)}, u32[]{:S(2)}, u32[]{:S(2)}) collective-permute-start(bf16[40,128]{1,0:T(8,128)(2,1)S(1)} %add_convert_fusion.whole), channel_id=1, source_target_pairs={{8,16},{0,24},{248,32},{240,40},{9,17},{1,25},{249,33},{241,41},{1... | collective-permute-start | bytes 30728 | tf_op jit(solution)/shard_map/ppermute | solution.py:234
  89.0 2.7 %collective-permute-start.10 = (bf16[40,128]{1,0:T(8,128)(2,1)S(1)}, bf16[40,128]{1,0:T(8,128)(2,1)S(1)}, u32[]{:S(2)}, u32[]{:S(2)}) collective-permute-start(bf16[40,128]{1,0:T(8,128)(2,1)S(1)} %add_convert_fusion.whole), channel_id=1, source_target_pairs={{8,48},{0,56},{248,64},{240,72},{9,49},{1,57},{249,65},{241,73},{1... | collective-permute-start | bytes 30728 | tf_op jit(solution)/shard_map/ppermute | solution.py:234
  90.4 1.3 %collective-permute-start.11 = (bf16[40,128]{1,0:T(8,128)(2,1)S(1)}, bf16[40,128]{1,0:T(8,128)(2,1)S(1)}, u32[]{:S(2)}, u32[]{:S(2)}) collective-permute-start(bf16[40,128]{1,0:T(8,128)(2,1)S(1)} %collective-permute-done.9.first), channel_id=1, source_target_pairs={{16,80},{24,88},{32,96},{40,104},{17,81},{25,89},{33,97},{41,105},... | collective-permute-start | bytes 30728 | tf_op jit(solution)/shard_map/ppermute | solution.py:234
  91.7 0.7 collective-permute-start.12
  92.4 0.7 collective-permute-start.13
